TPU v7x, 32 devices: a whole 2x2x4 slice. The times are simulated.
32 devices in a mesh: rep: 2 (over x), mp: 16 (over z, y, core).
Axes of the slice: x: 2, y: 2, z: 4, core: 2. Of those that a mesh axis runs over, the one named last changes fastest.
Arguments:
- tokens: bfloat16 [1280, 3072], P(('rep', 'mp')), may hold values from -6 to 6
- w_in: bfloat16 [2, 3072, 2, 12288], P('rep', None, None, 'mp'), may hold values from -0.109375 to 0.109375
- w_down: bfloat16 [2, 12288, 3072], P('rep', 'mp'), may hold values from -0.0546875 to 0.0546875
- norm_gain: float32 [3072], replicated, may hold values from 0.1 to 1.9
- final_gain: float32 [3072], replicated, may hold values from 0.1 to 1.9
- value_head: float32 [3072], replicated, may hold values from -0.6 to 0.6
- owner: int32 [16], P('mp'), may hold values from 0 to 1
- lengths: int32 [16], P('rep'), may hold values from 20 to 80, as said below
- offsets: int32 [16], P('rep'), may hold values from 0 to 620, as said below
Outputs:
- mixed: bfloat16 [1280, 3072], P(('rep', 'mp'))
- rewards: float32 [16], P('rep')
Inputs may be any that keep to these rules, and one draw needn't show every extreme that they name: `lengths`: every rollout is at least a quarter of 80 long; in each group one rollout has exactly 80 tokens. `offsets`: rollout j of a group lies wholly within slots j * 80 to (j + 1) * 80 - 1 of its group; the other slots are padding.
All inputs are finite; a program needn't handle non-finite values.
Results may differ from a plain program's by a relative error of at most 0.0046.
Values may be sent and summed in bfloat16 or wider, within the bound.
No kernel may reach another device: no remote copies, remote signals or barrier semaphores. Data moves between devices by JAX's collectives and lax.ppermute only.
A program may use at most 128 MiB of HBM per device.

v0:
```python
import functools

import jax
import jax.numpy as jnp
from jax import lax
from jax.experimental import pallas as pl
from jax.experimental.pallas import tpu as pltpu
from jax.sharding import PartitionSpec as P


AXES = ("rep", "mp")


def spread(value, axis, source):
    kept = jnp.where(lax.axis_index(axis) == source, value, 0).astype(value.dtype)
    return lax.psum(kept, axis)


def membership(slots, lengths, offsets):
    inside = (slots[:, None] >= offsets[None, :]) & (
        slots[:, None] < offsets[None, :] + lengths[None, :]
    )
    return inside.astype(jnp.float32)


def rms_normed(rows_f, gain):
    return rows_f * lax.rsqrt(jnp.mean(rows_f * rows_f, axis=1, keepdims=True) + 1e-06) * gain


def window_kernel(count, tile, owner_ref, *refs):
    owned = owner_ref[0] == lax.axis_index("rep")
    parts = refs[:count]
    in_ref, down_ref = refs[count : count + 2]
    outs = refs[count + 2 : 2 * count + 2]
    rows_ref, hidden_ref = refs[2 * count + 2 :]
    hidden, width = down_ref.shape
    spans = []
    start = 0
    for part in parts:
        spans.append((start, start + part.shape[0]))
        start += part.shape[0]

    @pl.when(owned)
    def _():
        for part, (low, high) in zip(parts, spans):
            rows_ref[low:high, :] = part[...]

        rows = rows_ref[...]
        for at in range(0, hidden, tile):
            gate = jnp.dot(rows, in_ref[:, at : at + tile], preferred_element_type=jnp.float32)
            up_at = hidden + at
            up = jnp.dot(
                rows, in_ref[:, up_at : up_at + tile], preferred_element_type=jnp.float32
            )
            hidden_ref[:, at : at + tile] = (jax.nn.gelu(gate, approximate=True) * up).astype(
                hidden_ref.dtype
            )
        wide = 2 * tile
        for at in range(0, width, wide):
            sums = jnp.dot(
                hidden_ref[...], down_ref[:, at : at + wide], preferred_element_type=jnp.float32
            )
            for out, (low, high) in zip(outs, spans):
                out[:, at : at + wide] = sums[low:high, :].astype(out.dtype)

    @pl.when(jnp.logical_not(owned))
    def _():
        for out in outs:
            out[...] = jnp.zeros_like(out)


def window(owner, parts, inner, outer):
    count = len(parts)
    rows = sum(part.shape[0] for part in parts)
    hidden, width = outer.shape
    tile = 256 if hidden % 256 == 0 else 128
    vmem = pl.BlockSpec(memory_space=pltpu.VMEM)
    return pl.pallas_call(
        functools.partial(window_kernel, count, tile),
        out_shape=[jax.ShapeDtypeStruct(part.shape, part.dtype) for part in parts],
        in_specs=[pl.BlockSpec(memory_space=pltpu.SMEM)] + [vmem] * (count + 2),
        out_specs=[vmem] * count,
        scratch_shapes=[
            pltpu.VMEM((rows, width), jnp.bfloat16),
            pltpu.VMEM((rows, hidden), jnp.bfloat16),
        ],
        compiler_params=pltpu.CompilerParams(
            vmem_limit_bytes=2 * (3 * rows * width + 2 * rows * hidden)
        ),
        cost_estimate=pl.CostEstimate(
            flops=6 * rows * width * hidden,
            bytes_accessed=4 * rows * width,
            transcendentals=rows * hidden,
        ),
        name="window",
    )(owner, *parts, inner, outer)


def finish(resid, final_gain, value_head):
    return jnp.dot(
        rms_normed(resid, final_gain), value_head, precision=lax.Precision.HIGHEST
    )


def add_f32(*terms):
    total = terms[0].astype(jnp.float32)
    for term in terms[1:]:
        total = total + term.astype(jnp.float32)
    return total


def norm_kernel(tokens_ref, gain_ref, out_ref):
    width = tokens_ref.shape[1]
    rows = tokens_ref[...].astype(jnp.float32)
    scale = lax.rsqrt(jnp.sum(rows * rows, axis=1, keepdims=True) / width + 1e-06)
    out_ref[...] = (rows * scale * gain_ref[...]).astype(out_ref.dtype)


def pick_kernel(x_ref, y_ref, *refs):
    out_ref = refs[-1]
    even = lax.axis_index("mp") % 2 == 0

    @pl.when(even)
    def _():
        out_ref[...] = y_ref[...]

    @pl.when(jnp.logical_not(even))
    def _():
        out_ref[...] = x_ref[...]


def stack_kernel(mine_ref, x_ref, y_ref, far_ref, out_ref):
    size = mine_ref.shape[0]
    for place, ref in enumerate((mine_ref, x_ref, y_ref, far_ref)):
        out_ref[place * size : (place + 1) * size] = ref[...]


def far_kernel(part_ref, back_ref, out_ref):
    low = 3 * out_ref.shape[0]
    out_ref[...] = add_f32(part_ref[low:], back_ref[low:]).astype(out_ref.dtype)


def near_kernel(part_ref, back_ref, far_ref, x_ref, y_ref):
    size = far_ref.shape[0]
    even = lax.axis_index("mp") % 2 == 0
    x_at, y_at = slice(size, 2 * size), slice(2 * size, 3 * size)
    for out, at, takes in ((x_ref, x_at, jnp.logical_not(even)), (y_ref, y_at, even)):

        @pl.when(takes)
        def _():
            out[...] = add_f32(part_ref[at], back_ref[at], far_ref[...]).astype(out.dtype)

        @pl.when(jnp.logical_not(takes))
        def _():
            out[...] = add_f32(part_ref[at], back_ref[at]).astype(out.dtype)


def own_kernel(part_ref, back_ref, x_ref, y_ref, out_ref):
    size = x_ref.shape[0]
    out_ref[...] = add_f32(
        part_ref[:size], back_ref[:size], x_ref[...], y_ref[...]
    ).astype(out_ref.dtype)


def local(kernel, args, shapes):
    vmem = pl.BlockSpec(memory_space=pltpu.VMEM)
    outs = [jax.ShapeDtypeStruct(shape, args[0].dtype) for shape in shapes]
    cost = 4 * args[0].size
    result = pl.pallas_call(
        kernel,
        out_shape=outs,
        in_specs=[vmem] * len(args),
        out_specs=[vmem] * len(outs),
        compiler_params=pltpu.CompilerParams(vmem_limit_bytes=4 << 20),
        cost_estimate=pl.CostEstimate(flops=cost, bytes_accessed=2 * cost, transcendentals=0),
    )(*args)
    return result if len(outs) > 1 else result[0]


def finish_kernel(count, size, lengths_ref, offsets_ref, tokens_ref, *refs):
    sums = refs[:count]
    gain_ref, head_ref, mixed_ref, totals_ref = refs[count:]
    width = tokens_ref.shape[1]
    delta = add_f32(*(part[...] for part in sums))
    slots = lax.axis_index("mp") * size + lax.broadcasted_iota(jnp.int32, (size, 1), 0)
    member = [
        jnp.where(
            (slots >= offsets_ref[seq]) & (slots < offsets_ref[seq] + lengths_ref[seq]), 1.0, 0.0
        )
        for seq in range(lengths_ref.shape[0])
    ]
    live = member[0]
    for column in member[1:]:
        live = live + column
    resid = tokens_ref[...].astype(jnp.float32) + delta * live
    mixed_ref[...] = resid.astype(mixed_ref.dtype)
    scale = lax.rsqrt(jnp.sum(resid * resid, axis=1, keepdims=True) / width + 1e-06)
    final = resid * scale * gain_ref[...]
    values = jnp.sum(final * head_ref[...], axis=1, keepdims=True)
    for seq, column in enumerate(member):
        total = jnp.sum(values * column, axis=0, keepdims=True)
        totals_ref[seq : seq + 1, :] = jnp.broadcast_to(total, (1, totals_ref.shape[1]))


def finish_rows(tokens, sums, final_gain, value_head, lengths, offsets):
    size, _ = tokens.shape
    smem = pl.BlockSpec(memory_space=pltpu.SMEM)
    vmem = pl.BlockSpec(memory_space=pltpu.VMEM)
    return pl.pallas_call(
        functools.partial(finish_kernel, len(sums), size),
        out_shape=[
            jax.ShapeDtypeStruct(tokens.shape, tokens.dtype),
            jax.ShapeDtypeStruct((lengths.shape[0], 128), jnp.float32),
        ],
        in_specs=[smem] * 2 + [vmem] * (len(sums) + 3),
        out_specs=[vmem] * 2,
        compiler_params=pltpu.CompilerParams(vmem_limit_bytes=8 << 20),
        cost_estimate=pl.CostEstimate(
            flops=10 * tokens.size, bytes_accessed=14 * tokens.size, transcendentals=size
        ),
        name="finish",
    )(lengths, offsets, tokens, *sums, final_gain[None, :], value_head[None, :])


def ready_kernel(later_ref, out_ref):
    out_ref[...] = jnp.zeros_like(out_ref)


def ready(later):
    return pl.pallas_call(
        ready_kernel,
        out_shape=jax.ShapeDtypeStruct((8, 128), jnp.float32),
        in_specs=[pl.BlockSpec(memory_space=pltpu.HBM)],
        out_specs=pl.BlockSpec(memory_space=pltpu.VMEM),
        compiler_params=pltpu.CompilerParams(
            vmem_limit_bytes=50 << 20, has_side_effects=True
        ),
        name="ready",
    )(later)


def tokens_travel(n_mp, tokens, w_in, w_down, norm_gain, final_gain, value_head, owner, lengths, offsets):
    size, width = tokens.shape
    hidden = w_in.shape[3]
    depth = n_mp // 4

    def permute(value, target):
        moves = []
        for rep in range(2):
            for mp in range(n_mp):
                to_rep, to_mp = target(rep, mp)
                moves.append((rep * n_mp + mp, to_rep * n_mp + to_mp))
        return lax.ppermute(value, AXES, moves)

    def to_core(value):
        return permute(value, lambda rep, mp: (rep, mp ^ 1))

    def to_x(value):
        return permute(value, lambda rep, mp: (1 - rep, mp))

    def to_y(value):
        return permute(value, lambda rep, mp: (rep, mp ^ 2))

    def to_turn(value):
        return permute(value, lambda rep, mp: (rep, mp ^ 2) if mp % 2 else (1 - rep, mp))

    def to_depth(value, step):
        return permute(value, lambda rep, mp: (rep, mp ^ (4 * step)))

    inner = w_in.reshape(width, 2 * hidden)
    outer = w_down.reshape(hidden, width)
    ready(inner)
    normed = local(norm_kernel, (tokens, norm_gain[None, :]), [tokens.shape])

    order = [0] + list(range(depth - 1, 0, -1))
    arrived = {0: normed}
    for step in order[1:]:
        arrived[step] = to_depth(normed, step)
    sums = {}
    for step in order:
        mine = arrived[step]
        from_x = to_x(mine)
        from_y = to_y(mine)
        held = () if step else (outer,)
        turn = local(pick_kernel, (from_x, from_y, *held), [(size, width)])
        far = to_turn(turn)
        block = local(stack_kernel, (mine, from_x, from_y, far), [(4 * size, width)])
        other = to_core(block)
        part, part_other = window(owner, [block, other], inner, outer)
        back = to_core(part_other)
        far = local(far_kernel, (part, back), [(size, width)])
        far = to_turn(far)
        x_sum, y_sum = local(near_kernel, (part, back, far), [(size, width)] * 2)
        x_sum = to_x(x_sum)
        y_sum = to_y(y_sum)
        total = local(own_kernel, (part, back, x_sum, y_sum), [(size, width)])
        sums[step] = to_depth(total, step) if step else total

    mixed, totals = finish_rows(
        tokens, [sums[step] for step in order], final_gain, value_head, lengths, offsets
    )
    totals = totals[:, 0]
    shares = jnp.broadcast_to(totals[None, :], (n_mp, totals.shape[0]))
    totals = jnp.sum(lax.all_to_all(shares, "mp", 0, 0, tiled=True), axis=0)
    return mixed, totals / lengths.astype(jnp.float32)


def weights_travel(tokens, w_in, w_down, norm_gain, final_gain, value_head, owner, lengths, offsets):
    owner_index = owner[0]
    tok_rows, width = tokens.shape
    hidden_cols = w_in.shape[3]
    tokens_f = tokens.astype(jnp.float32)
    normed = rms_normed(tokens_f, norm_gain).astype(jnp.bfloat16)
    inner = spread(w_in, "rep", owner_index).reshape(width, 2 * hidden_cols)
    outer = spread(w_down, "rep", owner_index).reshape(hidden_cols, width)
    piece = lax.all_gather(normed, "mp", axis=0, tiled=True)
    slots = jnp.arange(piece.shape[0], dtype=jnp.int32)
    products = jnp.dot(piece, inner, preferred_element_type=jnp.float32)
    live = jnp.sum(membership(slots, lengths, offsets), axis=1)[:, None]
    hidden = (
        jax.nn.gelu(products[:, :hidden_cols], approximate=True) * products[:, hidden_cols:] * live
    ).astype(jnp.bfloat16)
    delta = lax.psum_scatter(
        jnp.dot(hidden, outer, preferred_element_type=jnp.float32),
        "mp",
        scatter_dimension=0,
        tiled=True,
    )
    resid = tokens_f + delta
    values = finish(resid, final_gain, value_head)
    own_slots = lax.axis_index("mp") * tok_rows + jnp.arange(tok_rows, dtype=jnp.int32)
    member = membership(own_slots, lengths, offsets)
    totals = lax.psum(jnp.dot(values, member, precision=lax.Precision.HIGHEST), "mp")
    return resid.astype(jnp.bfloat16), totals / lengths.astype(jnp.float32)


def solution(mesh):
    n_rep, n_mp = mesh.shape["rep"], mesh.shape["mp"]
    pair = n_rep == 2 and n_mp % 4 == 0 and n_mp & (n_mp - 1) == 0
    body = functools.partial(tokens_travel, n_mp) if pair else weights_travel

    in_specs = (
        P(AXES, None),
        P("rep", None, None, "mp"),
        P("rep", "mp", None),
        P(),
        P(),
        P(),
        P("mp"),
        P("rep"),
        P("rep"),
    )
    return jax.shard_map(
        body, mesh=mesh, in_specs=in_specs, out_specs=(P(AXES, None), P("rep")), check_vma=False
    )
```

profile of v0, /device:TPU:0, one launch (start us, length us, event | category | flops | bytes accessed | tf_op | source)
XLA Modules:
  0.0 162.4 jit_solution(5084583216806756801)
XLA Ops:
  2.9 3.1 %collective-permute-start.28 = (bf16[40,3072]{1,0:T(8,128)(2,1)S(1)}, bf16[40,3072]{1,0:T(8,128)(2,1)S(1)}, u32[]{:S(2)}, u32[]{:S(2)}) collective-permute-start(bf16[40,3072]{1,0:T(8,128)(2,1)S(1)} %shard_map.104.mine_ref), channel_id=1, source_target_pairs={{0,4},{1,5},{2,6},{3,7},{4,0},{5,1},{6,2},{7,3},{8,12},{9,13},{10,... | collective-permute-start | bytes 737288 | tf_op jit(solution)/shard_map/ppermute | solution.py:253
  6.0 6.0 %collective-permute-done.28.mine_ref = bf16[40,3072]{1,0:T(8,128)(2,1)S(1)} collective-permute-done((bf16[40,3072]{1,0:T(8,128)(2,1)S(1)}, bf16[40,3072]{1,0:T(8,128)(2,1)S(1)}, u32[]{:S(2)}, u32[]{:S(2)}) %collective-permute-start.28) | collective-permute-done | bytes 245792 | tf_op jit(solution)/shard_map/ppermute | solution.py:253
  15.1 2.6 %collective-permute-start.18 = (bf16[40,3072]{1,0:T(8,128)(2,1)S(1)}, bf16[40,3072]{1,0:T(8,128)(2,1)S(1)}, u32[]{:S(2)}, u32[]{:S(2)}) collective-permute-start(bf16[40,3072]{1,0:T(8,128)(2,1)S(1)} %shard_map.104.mine_ref), channel_id=1, source_target_pairs={{0,8},{1,9},{2,10},{3,11},{4,12},{5,13},{6,14},{7,15},{8,0},{9,1},... | collective-permute-start | bytes 737288 | tf_op jit(solution)/shard_map/ppermute | solution.py:253
  20.9 6.7 %collective-permute-done.18.mine_ref = bf16[40,3072]{1,0:T(8,128)(2,1)S(1)} collective-permute-done((bf16[40,3072]{1,0:T(8,128)(2,1)S(1)}, bf16[40,3072]{1,0:T(8,128)(2,1)S(1)}, u32[]{:S(2)}, u32[]{:S(2)}) %collective-permute-start.18) | collective-permute-done | bytes 245792 | tf_op jit(solution)/shard_map/ppermute | solution.py:253
  28.7 3.4 %collective-permute-start.8 = (bf16[40,3072]{1,0:T(8,128)(2,1)S(1)}, bf16[40,3072]{1,0:T(8,128)(2,1)S(1)}, u32[]{:S(2)}, u32[]{:S(2)}) collective-permute-start(bf16[40,3072]{1,0:T(8,128)(2,1)S(1)} %shard_map.104.mine_ref), channel_id=1, source_target_pairs={{0,12},{1,13},{2,14},{3,15},{4,8},{5,9},{6,10},{7,11},{8,4},{9,5},... | collective-permute-start | bytes 737288 | tf_op jit(solution)/shard_map/ppermute | solution.py:253
  32.3 2.2 %collective-permute-done.19.x_ref = bf16[40,3072]{1,0:T(8,128)(2,1)S(1)} collective-permute-done((bf16[40,3072]{1,0:T(8,128)(2,1)S(1)}, bf16[40,3072]{1,0:T(8,128)(2,1)S(1)}, u32[]{:S(2)}, u32[]{:S(2)}) %collective-permute-start.19) | collective-permute-done | bytes 245792 | tf_op jit(solution)/shard_map/ppermute | solution.py:253
  49.0 2.5 %collective-permute-done.x_ref = bf16[40,3072]{1,0:T(8,128)(2,1)S(1)} collective-permute-done((bf16[40,3072]{1,0:T(8,128)(2,1)S(1)}, bf16[40,3072]{1,0:T(8,128)(2,1)S(1)}, u32[]{:S(2)}, u32[]{:S(2)}) %collective-permute-start) | collective-permute-done | bytes 245792 | tf_op jit(solution)/shard_map/ppermute | solution.py:253
  55.4 9.0 %copy.13 = bf16[384,8,2,768]{3,1,2,0:T(8,128)(2,1)} copy(bf16[384,8,2,768]{3,2,1,0:T(2,128)(2,1)} %bitcast.22) | data formatting | bytes 18874368
  67.6 3.7 %copy-done = bf16[384,8,2,768]{3,1,2,0:T(8,128)(2,1)S(1)} copy-done((bf16[384,8,2,768]{3,1,2,0:T(8,128)(2,1)S(1)}, bf16[384,8,2,768]{3,1,2,0:T(8,128)(2,1)}, u32[]{:S(2)}) %copy-start) | copy-done | bytes 9437208
  71.3 2.3 %copy-done.2 = bf16[1,768,3072]{2,1,0:T(8,128)(2,1)S(1)} copy-done((bf16[1,768,3072]{2,1,0:T(8,128)(2,1)S(1)}, bf16[1,768,3072]{2,1,0:T(8,128)(2,1)}, u32[]{:S(2)}) %copy-start.2) | copy-done | bytes 4718616
  73.7 6.0 %window.7 = (bf16[160,3072]{1,0:T(8,128)(2,1)S(1)}, bf16[160,3072]{1,0:T(8,128)(2,1)S(1)}) custom-call(s32[1]{0:T(128)S(6)} %copy.14.owner_ref, bf16[160,3072]{1,0:T(8,128)(2,1)S(1)} %shard_map.121.refs_0_, bf16[160,3072]{1,0:T(8,128)(2,1)} %collective-permute-done.32.refs_1_, bf16[3072,1536]{1,0:T(8,128)(2,1)S(1)} %bitcast.8, bf16[768,3072]{1,0:T(8,128)(2,1)S(1)} %bitcast.15), custom_call_target="tpu_custom_call" | custom-call | flops 4529848320 | bytes 3932160 | tf_op jit(solution)/shard_map/window/pallas_call | solution.py:78
  79.7 6.1 %window.6 = (bf16[160,3072]{1,0:T(8,128)(2,1)S(1)}, bf16[160,3072]{1,0:T(8,128)(2,1)S(1)}) custom-call(s32[1]{0:T(128)S(6)} %copy.14.owner_ref, bf16[160,3072]{1,0:T(8,128)(2,1)S(1)} %shard_map.116.refs_0_, bf16[160,3072]{1,0:T(8,128)(2,1)} %collective-permute-done.22.refs_1_, bf16[3072,1536]{1,0:T(8,128)(2,1)S(1)} %bitcast.9, bf16[768,3072]{1,0:T(8,128)(2,1)S(1)} %bitcast.16), custom_call_target="tpu_custom_call" | custom-call | flops 4529848320 | bytes 3932160 | tf_op jit(solution)/shard_map/window/pallas_call | solution.py:78
  86.4 6.0 %window.5 = (bf16[160,3072]{1,0:T(8,128)(2,1)S(1)}, bf16[160,3072]{1,0:T(8,128)(2,1)S(1)}) custom-call(s32[1]{0:T(128)S(6)} %copy.14.owner_ref, bf16[160,3072]{1,0:T(8,128)(2,1)S(1)} %shard_map.111.refs_0_, bf16[160,3072]{1,0:T(8,128)(2,1)} %collective-permute-done.12.refs_1_, bf16[3072,1536]{1,0:T(8,128)(2,1)S(1)} %bitcast.10, bf16[768,3072]{1,0:T(8,128)(2,1)S(1)} %bitcast.17), custom_call_target="tpu_custom_call" | custom-call | flops 4529848320 | bytes 3932160 | tf_op jit(solution)/shard_map/window/pallas_call | solution.py:78
  92.6 4.8 %window.4 = (bf16[160,3072]{1,0:T(8,128)(2,1)S(1)}, bf16[160,3072]{1,0:T(8,128)(2,1)S(1)}) custom-call(s32[1]{0:T(128)S(6)} %copy.14.owner_ref, bf16[160,3072]{1,0:T(8,128)(2,1)S(1)} %shard_map.106.refs_0_, bf16[160,3072]{1,0:T(8,128)(2,1)S(1)} %collective-permute-done.3.refs_1_, bf16[3072,1536]{1,0:T(8,128)(2,1)S(1)} %bitcast.13, bf16[768,3072]{1,0:T(8,128)(2,1)S(1)} %bitcast.18), custom_call_target="tpu_custom_call" | custom-call | flops 4529848320 | bytes 3932160 | tf_op jit(solution)/shard_map/window/pallas_call | solution.py:78
  107.6 5.0 %collective-permute-done.14.far_ref = bf16[40,3072]{1,0:T(8,128)(2,1)S(1)} collective-permute-done((bf16[40,3072]{1,0:T(8,128)(2,1)S(1)}, bf16[40,3072]{1,0:T(8,128)(2,1)S(1)}, u32[]{:S(2)}, u32[]{:S(2)}) %collective-permute-start.14) | collective-permute-done | bytes 245792 | tf_op jit(solution)/shard_map/ppermute | solution.py:253
  112.8 5.1 %collective-permute-done.5.far_ref = bf16[40,3072]{1,0:T(8,128)(2,1)S(1)} collective-permute-done((bf16[40,3072]{1,0:T(8,128)(2,1)S(1)}, bf16[40,3072]{1,0:T(8,128)(2,1)S(1)}, u32[]{:S(2)}, u32[]{:S(2)}) %collective-permute-start.5) | collective-permute-done | bytes 245792 | tf_op jit(solution)/shard_map/ppermute | solution.py:253
  117.9 5.3 %collective-permute-done.35.x_ref = bf16[40,3072]{1,0:T(8,128)(2,1)S(1)} collective-permute-done((bf16[40,3072]{1,0:T(8,128)(2,1)S(1)}, bf16[40,3072]{1,0:T(8,128)(2,1)S(1)}, u32[]{:S(2)}, u32[]{:S(2)}) %collective-permute-start.35) | collective-permute-done | bytes 245792 | tf_op jit(solution)/shard_map/ppermute | solution.py:253
  125.6 2.3 %collective-permute-done.25.x_ref = bf16[40,3072]{1,0:T(8,128)(2,1)S(1)} collective-permute-done((bf16[40,3072]{1,0:T(8,128)(2,1)S(1)}, bf16[40,3072]{1,0:T(8,128)(2,1)S(1)}, u32[]{:S(2)}, u32[]{:S(2)}) %collective-permute-start.25) | collective-permute-done | bytes 245792 | tf_op jit(solution)/shard_map/ppermute | solution.py:253
  128.0 4.8 %collective-permute-start.37 = (bf16[40,3072]{1,0:T(8,128)(2,1)S(1)}, bf16[40,3072]{1,0:T(8,128)(2,1)S(1)}, u32[]{:S(2)}, u32[]{:S(2)}) collective-permute-start(bf16[40,3072]{1,0:T(8,128)(2,1)S(1)} %shard_map.124), channel_id=1, source_target_pairs={{0,4},{1,5},{2,6},{3,7},{4,0},{5,1},{6,2},{7,3},{8,12},{9,13},{10,... | collective-permute-start | bytes 737288 | tf_op jit(solution)/shard_map/ppermute | solution.py:253
  133.1 4.0 %collective-permute-start.17 = (bf16[40,3072]{1,0:T(8,128)(2,1)S(1)}, bf16[40,3072]{1,0:T(8,128)(2,1)S(1)}, u32[]{:S(2)}, u32[]{:S(2)}) collective-permute-start(bf16[40,3072]{1,0:T(8,128)(2,1)S(1)} %shard_map.114), channel_id=1, source_target_pairs={{0,12},{1,13},{2,14},{3,15},{4,8},{5,9},{6,10},{7,11},{8,4},{9,5},... | collective-permute-start | bytes 737288 | tf_op jit(solution)/shard_map/ppermute | solution.py:253
  137.2 3.0 %collective-permute-done.37.refs_3_ = bf16[40,3072]{1,0:T(8,128)(2,1)S(1)} collective-permute-done((bf16[40,3072]{1,0:T(8,128)(2,1)S(1)}, bf16[40,3072]{1,0:T(8,128)(2,1)S(1)}, u32[]{:S(2)}, u32[]{:S(2)}) %collective-permute-start.37) | collective-permute-done | bytes 245792 | tf_op jit(solution)/shard_map/ppermute | solution.py:253
  140.2 7.4 %collective-permute-done.27.refs_2_ = bf16[40,3072]{1,0:T(8,128)(2,1)S(1)} collective-permute-done((bf16[40,3072]{1,0:T(8,128)(2,1)S(1)}, bf16[40,3072]{1,0:T(8,128)(2,1)S(1)}, u32[]{:S(2)}, u32[]{:S(2)}) %collective-permute-start.27) | collective-permute-done | bytes 245792 | tf_op jit(solution)/shard_map/ppermute | solution.py:253
  149.9 5.4 %all-to-all-start = ((f32[16,1,8]{2,1,0:T(1,128)}), f32[16,1,8]{2,1,0:T(1,128)S(1)}, u32[]{:S(2)}, u32[]{:S(2)}) async-start(f32[16,1,8]{2,1,0:T(1,128)} %broadcast_in_dim.20), calls=%async_computation | async-start | bytes 16384 | tf_op jit(solution)/shard_map/all_to_all | solution.py:304
  156.0 5.8 %all-to-all-done = f32[16,1,8]{2,1,0:T(1,128)S(1)} async-done(((f32[16,1,8]{2,1,0:T(1,128)}), f32[16,1,8]{2,1,0:T(1,128)S(1)}, u32[]{:S(2)}, u32[]{:S(2)}) %all-to-all-start) | async-done | bytes 544 | tf_op jit(solution)/shard_map/all_to_all | solution.py:304
  (117 shorter events, 48.3 us)
Async XLA Ops:
  15.1 12.4 %collective-permute-start.18 = (bf16[40,3072]{1,0:T(8,128)(2,1)S(1)}, bf16[40,3072]{1,0:T(8,128)(2,1)S(1)}, u32[]{:S(2)}, u32[]{:S(2)}) collective-permute-start(bf16[40,3072]{1,0:T(8,128)(2,1)S(1)} %shard_map.104.mine_ref), channel_id=1, source_target_pairs={{0,8},{1,9},{2,10},{3,11},{4,12},{5,13},{6,14},{7,15},{8,0},{9,1},... | collective-permute-start | bytes 737288 | tf_op jit(solution)/shard_map/ppermute | solution.py:253
  20.2 11.9 %collective-permute-start.31 = (bf16[40,3072]{1,0:T(8,128)(2,1)S(1)}, bf16[40,3072]{1,0:T(8,128)(2,1)S(1)}, u32[]{:S(2)}, u32[]{:S(2)}) collective-permute-start(bf16[40,3072]{1,0:T(8,128)(2,1)S(1)} %shard_map.120), channel_id=1, source_target_pairs={{0,16},{1,3},{2,18},{3,1},{4,20},{5,7},{6,22},{7,5},{8,24},{9,11},... | collective-permute-start | bytes 737288 | tf_op jit(solution)/shard_map/ppermute | solution.py:253
  32.2 35.5 %collective-permute-start.32 = (bf16[160,3072]{1,0:T(8,128)(2,1)S(1)}, bf16[160,3072]{1,0:T(8,128)(2,1)}, u32[]{:S(2)}, u32[]{:S(2)}) collective-permute-start(bf16[160,3072]{1,0:T(8,128)(2,1)S(1)} %shard_map.121.refs_0_), channel_id=1, source_target_pairs={{0,1},{1,0},{2,3},{3,2},{4,5},{5,4},{6,7},{7,6},{8,9},{9,8},{10,11... | collective-permute-start | bytes 2949128 | tf_op jit(solution)/shard_map/ppermute | solution.py:253
  41.9 37.9 %collective-permute-start.22 = (bf16[160,3072]{1,0:T(8,128)(2,1)S(1)}, bf16[160,3072]{1,0:T(8,128)(2,1)}, u32[]{:S(2)}, u32[]{:S(2)}) collective-permute-start(bf16[160,3072]{1,0:T(8,128)(2,1)S(1)} %shard_map.116.refs_0_), channel_id=1, source_target_pairs={{0,1},{1,0},{2,3},{3,2},{4,5},{5,4},{6,7},{7,6},{8,9},{9,8},{10,11... | collective-permute-start | bytes 2949128 | tf_op jit(solution)/shard_map/ppermute | solution.py:253
  41.9 9.6 %collective-permute-start = (bf16[40,3072]{1,0:T(8,128)(2,1)S(1)}, bf16[40,3072]{1,0:T(8,128)(2,1)S(1)}, u32[]{:S(2)}, u32[]{:S(2)}) collective-permute-start(bf16[40,3072]{1,0:T(8,128)(2,1)S(1)} %shard_map.104.mine_ref), channel_id=1, source_target_pairs={{0,16},{1,17},{2,18},{3,19},{4,20},{5,21},{6,22},{7,23},{8,24},{9,... | collective-permute-start | bytes 737288 | tf_op jit(solution)/shard_map/ppermute | solution.py:253
  53.7 11.4 %collective-permute-start.2 = (bf16[40,3072]{1,0:T(8,128)(2,1)}, bf16[40,3072]{1,0:T(8,128)(2,1)}, u32[]{:S(2)}, u32[]{:S(2)}) collective-permute-start(bf16[40,3072]{1,0:T(8,128)(2,1)} %shard_map.105), channel_id=1, source_target_pairs={{0,16},{1,3},{2,18},{3,1},{4,20},{5,7},{6,22},{7,5},{8,24},{9,11},... | collective-permute-start | bytes 737288 | tf_op jit(solution)/shard_map/ppermute | solution.py:253
  55.4 31.1 %collective-permute-start.12 = (bf16[160,3072]{1,0:T(8,128)(2,1)S(1)}, bf16[160,3072]{1,0:T(8,128)(2,1)}, u32[]{:S(2)}, u32[]{:S(2)}) collective-permute-start(bf16[160,3072]{1,0:T(8,128)(2,1)S(1)} %shard_map.111.refs_0_), channel_id=1, source_target_pairs={{0,1},{1,0},{2,3},{3,2},{4,5},{5,4},{6,7},{7,6},{8,9},{9,8},{10,11... | collective-permute-start | bytes 2949128 | tf_op jit(solution)/shard_map/ppermute | solution.py:253
  67.1 25.5 %collective-permute-start.3 = (bf16[160,3072]{1,0:T(8,128)(2,1)S(1)}, bf16[160,3072]{1,0:T(8,128)(2,1)S(1)}, u32[]{:S(2)}, u32[]{:S(2)}) collective-permute-start(bf16[160,3072]{1,0:T(8,128)(2,1)S(1)} %shard_map.106.refs_0_), channel_id=1, source_target_pairs={{0,1},{1,0},{2,3},{3,2},{4,5},{5,4},{6,7},{7,6},{8,9},{9,8},{10,11... | collective-permute-start | bytes 2949128 | tf_op jit(solution)/shard_map/ppermute | solution.py:253
  79.6 18.2 %collective-permute-start.33 = (bf16[160,3072]{1,0:T(8,128)(2,1)S(1)}, bf16[160,3072]{1,0:T(8,128)(2,1)S(1)}, u32[]{:S(2)}, u32[]{:S(2)}) collective-permute-start(bf16[160,3072]{1,0:T(8,128)(2,1)S(1)} %get-tuple-element.33), channel_id=1, source_target_pairs={{0,1},{1,0},{2,3},{3,2},{4,5},{5,4},{6,7},{7,6},{8,9},{9,8},{10,11... | collective-permute-start | bytes 2949128 | tf_op jit(solution)/shard_map/ppermute | solution.py:253
  85.9 12.1 %collective-permute-start.23 = (bf16[160,3072]{1,0:T(8,128)(2,1)S(1)}, bf16[160,3072]{1,0:T(8,128)(2,1)S(1)}, u32[]{:S(2)}, u32[]{:S(2)}) collective-permute-start(bf16[160,3072]{1,0:T(8,128)(2,1)S(1)} %get-tuple-element.29), channel_id=1, source_target_pairs={{0,1},{1,0},{2,3},{3,2},{4,5},{5,4},{6,7},{7,6},{8,9},{9,8},{10,11... | collective-permute-start | bytes 2949128 | tf_op jit(solution)/shard_map/ppermute | solution.py:253
  98.1 9.3 %collective-permute-start.24 = (bf16[40,3072]{1,0:T(8,128)(2,1)S(1)}, bf16[40,3072]{1,0:T(8,128)(2,1)S(1)}, u32[]{:S(2)}, u32[]{:S(2)}) collective-permute-start(bf16[40,3072]{1,0:T(8,128)(2,1)S(1)} %shard_map.117), channel_id=1, source_target_pairs={{0,16},{1,3},{2,18},{3,1},{4,20},{5,7},{6,22},{7,5},{8,24},{9,11},... | collective-permute-start | bytes 737288 | tf_op jit(solution)/shard_map/ppermute | solution.py:253
  100.2 12.4 %collective-permute-start.14 = (bf16[40,3072]{1,0:T(8,128)(2,1)S(1)}, bf16[40,3072]{1,0:T(8,128)(2,1)S(1)}, u32[]{:S(2)}, u32[]{:S(2)}) collective-permute-start(bf16[40,3072]{1,0:T(8,128)(2,1)S(1)} %shard_map.112), channel_id=1, source_target_pairs={{0,16},{1,3},{2,18},{3,1},{4,20},{5,7},{6,22},{7,5},{8,24},{9,11},... | collective-permute-start | bytes 737288 | tf_op jit(solution)/shard_map/ppermute | solution.py:253
  100.5 17.5 %collective-permute-start.5 = (bf16[40,3072]{1,0:T(8,128)(2,1)S(1)}, bf16[40,3072]{1,0:T(8,128)(2,1)S(1)}, u32[]{:S(2)}, u32[]{:S(2)}) collective-permute-start(bf16[40,3072]{1,0:T(8,128)(2,1)S(1)} %shard_map.107), channel_id=1, source_target_pairs={{0,16},{1,3},{2,18},{3,1},{4,20},{5,7},{6,22},{7,5},{8,24},{9,11},... | collective-permute-start | bytes 737288 | tf_op jit(solution)/shard_map/ppermute | solution.py:253
  104.4 18.8 %collective-permute-start.35 = (bf16[40,3072]{1,0:T(8,128)(2,1)S(1)}, bf16[40,3072]{1,0:T(8,128)(2,1)S(1)}, u32[]{:S(2)}, u32[]{:S(2)}) collective-permute-start(bf16[40,3072]{1,0:T(8,128)(2,1)S(1)} %get-tuple-element.34), channel_id=1, source_target_pairs={{0,16},{1,17},{2,18},{3,19},{4,20},{5,21},{6,22},{7,23},{8,24},{9,... | collective-permute-start | bytes 737288 | tf_op jit(solution)/shard_map/ppermute | solution.py:253
  104.4 18.9 %collective-permute-start.36 = (bf16[40,3072]{1,0:T(8,128)(2,1)S(1)}, bf16[40,3072]{1,0:T(8,128)(2,1)S(1)}, u32[]{:S(2)}, u32[]{:S(2)}) collective-permute-start(bf16[40,3072]{1,0:T(8,128)(2,1)S(1)} %get-tuple-element.35), channel_id=1, source_target_pairs={{0,2},{1,3},{2,0},{3,1},{4,6},{5,7},{6,4},{7,5},{8,10},{9,11},{10,... | collective-permute-start | bytes 737288 | tf_op jit(solution)/shard_map/ppermute | solution.py:253
  107.6 20.4 %collective-permute-start.25 = (bf16[40,3072]{1,0:T(8,128)(2,1)S(1)}, bf16[40,3072]{1,0:T(8,128)(2,1)S(1)}, u32[]{:S(2)}, u32[]{:S(2)}) collective-permute-start(bf16[40,3072]{1,0:T(8,128)(2,1)S(1)} %get-tuple-element.30), channel_id=1, source_target_pairs={{0,16},{1,17},{2,18},{3,19},{4,20},{5,21},{6,22},{7,23},{8,24},{9,... | collective-permute-start | bytes 737288 | tf_op jit(solution)/shard_map/ppermute | solution.py:253
  112.7 15.3 %collective-permute-start.26 = (bf16[40,3072]{1,0:T(8,128)(2,1)S(1)}, bf16[40,3072]{1,0:T(8,128)(2,1)S(1)}, u32[]{:S(2)}, u32[]{:S(2)}) collective-permute-start(bf16[40,3072]{1,0:T(8,128)(2,1)S(1)} %get-tuple-element.31), channel_id=1, source_target_pairs={{0,2},{1,3},{2,0},{3,1},{4,6},{5,7},{6,4},{7,5},{8,10},{9,11},{10,... | collective-permute-start | bytes 737288 | tf_op jit(solution)/shard_map/ppermute | solution.py:253
  117.9 14.9 %collective-permute-start.15 = (bf16[40,3072]{1,0:T(8,128)(2,1)S(1)}, bf16[40,3072]{1,0:T(8,128)(2,1)S(1)}, u32[]{:S(2)}, u32[]{:S(2)}) collective-permute-start(bf16[40,3072]{1,0:T(8,128)(2,1)S(1)} %get-tuple-element.26), channel_id=1, source_target_pairs={{0,16},{1,17},{2,18},{3,19},{4,20},{5,21},{6,22},{7,23},{8,24},{9,... | collective-permute-start | bytes 737288 | tf_op jit(solution)/shard_map/ppermute | solution.py:253
  123.2 9.8 %collective-permute-start.16 = (bf16[40,3072]{1,0:T(8,128)(2,1)S(1)}, bf16[40,3072]{1,0:T(8,128)(2,1)S(1)}, u32[]{:S(2)}, u32[]{:S(2)}) collective-permute-start(bf16[40,3072]{1,0:T(8,128)(2,1)S(1)} %get-tuple-element.27), channel_id=1, source_target_pairs={{0,2},{1,3},{2,0},{3,1},{4,6},{5,7},{6,4},{7,5},{8,10},{9,11},{10,... | collective-permute-start | bytes 737288 | tf_op jit(solution)/shard_map/ppermute | solution.py:253
  123.4 13.7 %collective-permute-start.6 = (bf16[40,3072]{1,0:T(8,128)(2,1)S(1)}, bf16[40,3072]{1,0:T(8,128)(2,1)S(1)}, u32[]{:S(2)}, u32[]{:S(2)}) collective-permute-start(bf16[40,3072]{1,0:T(8,128)(2,1)S(1)} %get-tuple-element.22), channel_id=1, source_target_pairs={{0,16},{1,17},{2,18},{3,19},{4,20},{5,21},{6,22},{7,23},{8,24},{9,... | collective-permute-start | bytes 737288 | tf_op jit(solution)/shard_map/ppermute | solution.py:253
  128.0 12.3 %collective-permute-start.37 = (bf16[40,3072]{1,0:T(8,128)(2,1)S(1)}, bf16[40,3072]{1,0:T(8,128)(2,1)S(1)}, u32[]{:S(2)}, u32[]{:S(2)}) collective-permute-start(bf16[40,3072]{1,0:T(8,128)(2,1)S(1)} %shard_map.124), channel_id=1, source_target_pairs={{0,4},{1,5},{2,6},{3,7},{4,0},{5,1},{6,2},{7,3},{8,12},{9,13},{10,... | collective-permute-start | bytes 737288 | tf_op jit(solution)/shard_map/ppermute | solution.py:253
  132.9 14.7 %collective-permute-start.27 = (bf16[40,3072]{1,0:T(8,128)(2,1)S(1)}, bf16[40,3072]{1,0:T(8,128)(2,1)S(1)}, u32[]{:S(2)}, u32[]{:S(2)}) collective-permute-start(bf16[40,3072]{1,0:T(8,128)(2,1)S(1)} %shard_map.119), channel_id=1, source_target_pairs={{0,8},{1,9},{2,10},{3,11},{4,12},{5,13},{6,14},{7,15},{8,0},{9,1},... | collective-permute-start | bytes 737288 | tf_op jit(solution)/shard_map/ppermute | solution.py:253
  133.1 14.5 %collective-permute-start.17 = (bf16[40,3072]{1,0:T(8,128)(2,1)S(1)}, bf16[40,3072]{1,0:T(8,128)(2,1)S(1)}, u32[]{:S(2)}, u32[]{:S(2)}) collective-permute-start(bf16[40,3072]{1,0:T(8,128)(2,1)S(1)} %shard_map.114), channel_id=1, source_target_pairs={{0,12},{1,13},{2,14},{3,15},{4,8},{5,9},{6,10},{7,11},{8,4},{9,5},... | collective-permute-start | bytes 737288 | tf_op jit(solution)/shard_map/ppermute | solution.py:253
  149.9 11.9 %all-to-all-start = ((f32[16,1,8]{2,1,0:T(1,128)}), f32[16,1,8]{2,1,0:T(1,128)S(1)}, u32[]{:S(2)}, u32[]{:S(2)}) async-start(f32[16,1,8]{2,1,0:T(1,128)} %broadcast_in_dim.20), calls=%async_computation | async-start | bytes 16384 | tf_op jit(solution)/shard_map/all_to_all | solution.py:304
  (30 other events, 441.7 us)
where the time goes:
time: 163 us; the launch traced here: 162 us
  waiting for transfers between devices  62.7 us (38%)
  starting transfers between devices  50 us (31%)
  Pallas kernels  28.6 us (18%)
  local copies, waits for them, and re-layouts  18.8 us (12%)
  between operations  1.71 us (1%)
    ppermute x38, waiting for transfers between devices, permute(): return lax.ppermute(value, AXES, moves)  56.9 us
    ppermute x38, starting transfers between devices, permute(): return lax.ppermute(value, AXES, moves)  44.6 us
    pallas_call x4, Pallas kernels, window(): pl.pallas_call(functools.partial(window_kernel, count, tile), out_shape=[...  22.9 us
    unnamed x31, local copies, waits for them, and re-layouts  18.1 us
    all_to_all x1, waiting for transfers between devices, tokens_travel(): totals = jnp.sum(lax.all_to_all(shares, 'mp', 0, 0, tiled=True), axis=0)  5.83 us
    all_to_all x1, starting transfers between devices, tokens_travel(): totals = jnp.sum(lax.all_to_all(shares, 'mp', 0, 0, tiled=True), axis=0)  5.42 us
    pallas_call x21, Pallas kernels, local(): pl.pallas_call(kernel, out_shape=outs, in_specs=[vmem] * len(args), out_s...  3.51 us
  transfers between devices with their start and end apart: 39, of which 21 were waited for; matrix products, arithmetic and copies ran while one was open for 6% of the time, Pallas kernels for 17%

commit v1 on v0

--- a/solution.py
+++ b/solution.py
@@ -9,6 +9,8 @@
 
 
 AXES = ("rep", "mp")
+RELAYS = 4
+RELAY_GRANT = 53_000_000
 
 
 def spread(value, axis, source):
@@ -30,9 +32,9 @@
 def window_kernel(count, tile, owner_ref, *refs):
     owned = owner_ref[0] == lax.axis_index("rep")
     parts = refs[:count]
-    in_ref, down_ref = refs[count : count + 2]
-    outs = refs[count + 2 : 2 * count + 2]
-    rows_ref, hidden_ref = refs[2 * count + 2 :]
+    outs = refs[-count - 2 : -2]
+    rows_ref, hidden_ref = refs[-2:]
+    in_refs, down_ref = refs[count : -count - 3], refs[-count - 3]
     hidden, width = down_ref.shape
     spans = []
     start = 0
@@ -45,13 +47,20 @@
         for part, (low, high) in zip(parts, spans):
             rows_ref[low:high, :] = part[...]
 
-        rows = rows_ref[...]
+        def product(at):
+            total = None
+            for place, in_ref in enumerate(in_refs):
+                depth = in_ref.shape[0]
+                term = jnp.dot(
+                    rows_ref[:, place * depth : (place + 1) * depth],
+                    in_ref[:, at : at + tile],
+                    preferred_element_type=jnp.float32,
+                )
+                total = term if total is None else total + term
+            return total
+
         for at in range(0, hidden, tile):
-            gate = jnp.dot(rows, in_ref[:, at : at + tile], preferred_element_type=jnp.float32)
-            up_at = hidden + at
-            up = jnp.dot(
-                rows, in_ref[:, up_at : up_at + tile], preferred_element_type=jnp.float32
-            )
+            gate, up = product(at), product(hidden + at)
             hidden_ref[:, at : at + tile] = (jax.nn.gelu(gate, approximate=True) * up).astype(
                 hidden_ref.dtype
             )
@@ -78,7 +87,7 @@
     return pl.pallas_call(
         functools.partial(window_kernel, count, tile),
         out_shape=[jax.ShapeDtypeStruct(part.shape, part.dtype) for part in parts],
-        in_specs=[pl.BlockSpec(memory_space=pltpu.SMEM)] + [vmem] * (count + 2),
+        in_specs=[pl.BlockSpec(memory_space=pltpu.SMEM)] + [vmem] * (count + len(inner) + 1),
         out_specs=[vmem] * count,
         scratch_shapes=[
             pltpu.VMEM((rows, width), jnp.bfloat16),
@@ -93,7 +102,7 @@
             transcendentals=rows * hidden,
         ),
         name="window",
-    )(owner, *parts, inner, outer)
+    )(owner, *parts, *inner, outer)
 
 
 def finish(resid, final_gain, value_head):
@@ -222,21 +231,40 @@
     )(lengths, offsets, tokens, *sums, final_gain[None, :], value_head[None, :])
 
 
-def ready_kernel(later_ref, out_ref):
-    out_ref[...] = jnp.zeros_like(out_ref)
-
-
-def ready(later):
+def relay_kernel(start, in_ref, out_ref, held_ref, sems):
+    blocks, rows = held_ref.shape[0], held_ref.shape[1]
+    loads = [
+        pltpu.make_async_copy(
+            in_ref.at[0, pl.ds(start + block * rows, rows)], held_ref.at[block], sems.at[block]
+        )
+        for block in range(blocks)
+    ]
+    for copy in loads:
+        copy.start()
+    for block, copy in enumerate(loads):
+        copy.wait()
+        out_ref[block * rows : (block + 1) * rows, :] = held_ref[block].reshape(
+            rows, out_ref.shape[1]
+        )
+
+
+def relay(w_in, start, size, grant):
+    _, _, sides, hidden = w_in.shape
+    rows = 128 if size % 128 == 0 else size
+    held = 2 * size * sides * hidden
     return pl.pallas_call(
-        ready_kernel,
-        out_shape=jax.ShapeDtypeStruct((8, 128), jnp.float32),
+        functools.partial(relay_kernel, start),
+        out_shape=jax.ShapeDtypeStruct((size, sides * hidden), w_in.dtype),
         in_specs=[pl.BlockSpec(memory_space=pltpu.HBM)],
         out_specs=pl.BlockSpec(memory_space=pltpu.VMEM),
-        compiler_params=pltpu.CompilerParams(
-            vmem_limit_bytes=50 << 20, has_side_effects=True
-        ),
-        name="ready",
-    )(later)
+        scratch_shapes=[
+            pltpu.VMEM((size // rows, rows, sides, hidden), w_in.dtype),
+            pltpu.SemaphoreType.DMA((size // rows,)),
+        ],
+        compiler_params=pltpu.CompilerParams(vmem_limit_bytes=grant),
+        cost_estimate=pl.CostEstimate(flops=held, bytes_accessed=2 * held, transcendentals=0),
+        name="relay",
+    )(w_in)
 
 
 def tokens_travel(n_mp, tokens, w_in, w_down, norm_gain, final_gain, value_head, owner, lengths, offsets):
@@ -267,9 +295,13 @@
     def to_depth(value, step):
         return permute(value, lambda rep, mp: (rep, mp ^ (4 * step)))
 
-    inner = w_in.reshape(width, 2 * hidden)
     outer = w_down.reshape(hidden, width)
-    ready(inner)
+    depth_cut = width // RELAYS
+    grant = RELAY_GRANT
+    inner = []
+    for piece in range(RELAYS):
+        inner.append(relay(w_in, piece * depth_cut, depth_cut, grant))
+        grant -= 4 * depth_cut * hidden
     normed = local(norm_kernel, (tokens, norm_gain[None, :]), [tokens.shape])
 
     order = [0] + list(range(depth - 1, 0, -1))

time: 163 us -> 149 us (0.914)
  local copies, waits for them, and re-layouts: 18.8 us -> 1.81 us
  blocking collectives: 0 us -> 11.3 us
  waiting for transfers between devices: 62.7 us -> 57.1 us
  starting transfers between devices: 50 us -> 44.6 us
  Pallas kernels: 28.6 us -> 31.2 us
    unnamed x31 -> x16, local copies, waits for them, and re-layouts: 18.1 us -> 1.68 us
    all_to_all x0 -> x1, blocking collectives: none -> 11.3 us  [tokens_travel(): totals = jnp.sum(lax.all_to_all(shares, 'mp', 0, 0, tiled=True), axis=0)]
    pallas_call x1 -> x4, Pallas kernels: 0.59 us -> 7.11 us  [relay(): pl.pallas_call(functools.partial(relay_kernel, start), out_shape=jax.Shap...]
    all_to_all x1 -> x0, waiting for transfers between devices: 5.83 us -> none  [tokens_travel(): totals = jnp.sum(lax.all_to_all(shares, 'mp', 0, 0, tiled=True), axis=0)]
    all_to_all x1 -> x0, starting transfers between devices: 5.42 us -> none  [tokens_travel(): totals = jnp.sum(lax.all_to_all(shares, 'mp', 0, 0, tiled=True), axis=0)]
    pallas_call x4, Pallas kernels: 22.9 us -> 20.5 us  [window(): pl.pallas_call(functools.partial(window_kernel, count, tile), out_shape=[...]
  transfers between devices with their start and end apart: 39 -> 38, of which waited for: 21 -> 20; matrix products, arithmetic and copies ran while one was open for 6% -> 0% of each run, Pallas kernels for 17% -> 20%
where the time goes in v1:
time: 149 us; the launch traced here: 148 us
  waiting for transfers between devices  57.1 us (38%)
  starting transfers between devices  44.6 us (30%)
  Pallas kernels  31.2 us (21%)
  blocking collectives  11.3 us (8%)
  local copies, waits for them, and re-layouts  1.81 us (1%)
  between operations  1.66 us (1%)
    ppermute x38, waiting for transfers between devices, permute(): return lax.ppermute(value, AXES, moves)  57.1 us
    ppermute x38, starting transfers between devices, permute(): return lax.ppermute(value, AXES, moves)  44.6 us
    pallas_call x4, Pallas kernels, window(): pl.pallas_call(functools.partial(window_kernel, count, tile), out_shape=[...  20.5 us
    all_to_all x1, blocking collectives, tokens_travel(): totals = jnp.sum(lax.all_to_all(shares, 'mp', 0, 0, tiled=True), axis=0)  11.3 us
    pallas_call x4, Pallas kernels, relay(): pl.pallas_call(functools.partial(relay_kernel, start), out_shape=jax.Shap...  7.11 us
  transfers between devices with their start and end apart: 38, of which 20 were waited for; matrix products, arithmetic and copies ran while one was open for 0% of the time, Pallas kernels for 20%

profile of v1, /device:TPU:0, one launch (start us, length us, event | category | flops | bytes accessed | tf_op | source)
XLA Modules:
  0.0 148.2 jit_solution(2594983086505150995)
XLA Ops:
  2.4 3.1 %collective-permute-start.28 = (bf16[40,3072]{1,0:T(8,128)(2,1)S(1)}, bf16[40,3072]{1,0:T(8,128)(2,1)S(1)}, u32[]{:S(2)}, u32[]{:S(2)}) collective-permute-start(bf16[40,3072]{1,0:T(8,128)(2,1)S(1)} %shard_map.104.mine_ref), channel_id=1, source_target_pairs={{0,4},{1,5},{2,6},{3,7},{4,0},{5,1},{6,2},{7,3},{8,12},{9,13},{10,... | collective-permute-start | bytes 737288 | tf_op jit(solution)/shard_map/ppermute | solution.py:281
  5.6 6.0 %collective-permute-done.28.mine_ref = bf16[40,3072]{1,0:T(8,128)(2,1)S(1)} collective-permute-done((bf16[40,3072]{1,0:T(8,128)(2,1)S(1)}, bf16[40,3072]{1,0:T(8,128)(2,1)S(1)}, u32[]{:S(2)}, u32[]{:S(2)}) %collective-permute-start.28) | collective-permute-done | bytes 245792 | tf_op jit(solution)/shard_map/ppermute | solution.py:281
  14.7 2.6 %collective-permute-start.18 = (bf16[40,3072]{1,0:T(8,128)(2,1)S(1)}, bf16[40,3072]{1,0:T(8,128)(2,1)S(1)}, u32[]{:S(2)}, u32[]{:S(2)}) collective-permute-start(bf16[40,3072]{1,0:T(8,128)(2,1)S(1)} %shard_map.104.mine_ref), channel_id=1, source_target_pairs={{0,8},{1,9},{2,10},{3,11},{4,12},{5,13},{6,14},{7,15},{8,0},{9,1},... | collective-permute-start | bytes 737288 | tf_op jit(solution)/shard_map/ppermute | solution.py:281
  20.5 6.7 %collective-permute-done.18.mine_ref = bf16[40,3072]{1,0:T(8,128)(2,1)S(1)} collective-permute-done((bf16[40,3072]{1,0:T(8,128)(2,1)S(1)}, bf16[40,3072]{1,0:T(8,128)(2,1)S(1)}, u32[]{:S(2)}, u32[]{:S(2)}) %collective-permute-start.18) | collective-permute-done | bytes 245792 | tf_op jit(solution)/shard_map/ppermute | solution.py:281
  28.3 3.4 %collective-permute-start.8 = (bf16[40,3072]{1,0:T(8,128)(2,1)S(1)}, bf16[40,3072]{1,0:T(8,128)(2,1)S(1)}, u32[]{:S(2)}, u32[]{:S(2)}) collective-permute-start(bf16[40,3072]{1,0:T(8,128)(2,1)S(1)} %shard_map.104.mine_ref), channel_id=1, source_target_pairs={{0,12},{1,13},{2,14},{3,15},{4,8},{5,9},{6,10},{7,11},{8,4},{9,5},... | collective-permute-start | bytes 737288 | tf_op jit(solution)/shard_map/ppermute | solution.py:281
  31.8 2.2 %collective-permute-done.19.x_ref = bf16[40,3072]{1,0:T(8,128)(2,1)S(1)} collective-permute-done((bf16[40,3072]{1,0:T(8,128)(2,1)S(1)}, bf16[40,3072]{1,0:T(8,128)(2,1)S(1)}, u32[]{:S(2)}, u32[]{:S(2)}) %collective-permute-start.19) | collective-permute-done | bytes 245792 | tf_op jit(solution)/shard_map/ppermute | solution.py:281
  48.6 2.5 %collective-permute-done.x_ref = bf16[40,3072]{1,0:T(8,128)(2,1)S(1)} collective-permute-done((bf16[40,3072]{1,0:T(8,128)(2,1)S(1)}, bf16[40,3072]{1,0:T(8,128)(2,1)S(1)}, u32[]{:S(2)}, u32[]{:S(2)}) %collective-permute-start) | collective-permute-done | bytes 245792 | tf_op jit(solution)/shard_map/ppermute | solution.py:281
  62.8 4.8 %window.7 = (bf16[160,3072]{1,0:T(8,128)(2,1)S(1)}, bf16[160,3072]{1,0:T(8,128)(2,1)S(1)}) custom-call(s32[1]{0:T(128)S(6)} %copy.13.owner_ref, bf16[160,3072]{1,0:T(8,128)(2,1)S(1)} %shard_map.121.refs_0_, bf16[160,3072]{1,0:T(8,128)(2,1)S(1)} %collective-permute-done.32.refs_1_, bf16[768,1536]{1,0:T(8,128)(2,1)S(1)} %relay.4.refs_2_, ...), custom_call_target="tpu_custom_call" | custom-call | flops 4529848320 | bytes 3932160 | tf_op jit(solution)/shard_map/window/pallas_call | solution.py:87
  67.6 5.0 %window.6 = (bf16[160,3072]{1,0:T(8,128)(2,1)S(1)}, bf16[160,3072]{1,0:T(8,128)(2,1)S(1)}) custom-call(s32[1]{0:T(128)S(6)} %copy.13.owner_ref, bf16[160,3072]{1,0:T(8,128)(2,1)S(1)} %shard_map.116.refs_0_, bf16[160,3072]{1,0:T(8,128)(2,1)S(1)} %collective-permute-done.22.refs_1_, bf16[768,1536]{1,0:T(8,128)(2,1)S(1)} %relay.4.refs_2_, ...), custom_call_target="tpu_custom_call" | custom-call | flops 4529848320 | bytes 3932160 | tf_op jit(solution)/shard_map/window/pallas_call | solution.py:87
  73.0 6.0 %window.5 = (bf16[160,3072]{1,0:T(8,128)(2,1)S(1)}, bf16[160,3072]{1,0:T(8,128)(2,1)S(1)}) custom-call(s32[1]{0:T(128)S(6)} %copy.13.owner_ref, bf16[160,3072]{1,0:T(8,128)(2,1)S(1)} %shard_map.111.refs_0_, bf16[160,3072]{1,0:T(8,128)(2,1)} %collective-permute-done.12.refs_1_, bf16[768,1536]{1,0:T(8,128)(2,1)S(1)} %relay.4.refs_2_, ...), custom_call_target="tpu_custom_call" | custom-call | flops 4529848320 | bytes 3932160 | tf_op jit(solution)/shard_map/window/pallas_call | solution.py:87
  79.2 4.8 %window.4 = (bf16[160,3072]{1,0:T(8,128)(2,1)S(1)}, bf16[160,3072]{1,0:T(8,128)(2,1)S(1)}) custom-call(s32[1]{0:T(128)S(6)} %copy.13.owner_ref, bf16[160,3072]{1,0:T(8,128)(2,1)S(1)} %shard_map.106.refs_0_, bf16[160,3072]{1,0:T(8,128)(2,1)S(1)} %collective-permute-done.3.refs_1_, bf16[768,1536]{1,0:T(8,128)(2,1)S(1)} %relay.4.refs_2_, ...), custom_call_target="tpu_custom_call" | custom-call | flops 4529848320 | bytes 3932160 | tf_op jit(solution)/shard_map/window/pallas_call | solution.py:87
  84.6 2.1 %collective-permute-start.24 = (bf16[40,3072]{1,0:T(8,128)(2,1)S(1)}, bf16[40,3072]{1,0:T(8,128)(2,1)S(1)}, u32[]{:S(2)}, u32[]{:S(2)}) collective-permute-start(bf16[40,3072]{1,0:T(8,128)(2,1)S(1)} %shard_map.117), channel_id=1, source_target_pairs={{0,16},{1,3},{2,18},{3,1},{4,20},{5,7},{6,22},{7,5},{8,24},{9,11},... | collective-permute-start | bytes 737288 | tf_op jit(solution)/shard_map/ppermute | solution.py:281
  86.9 2.1 %collective-permute-start.5 = (bf16[40,3072]{1,0:T(8,128)(2,1)S(1)}, bf16[40,3072]{1,0:T(8,128)(2,1)S(1)}, u32[]{:S(2)}, u32[]{:S(2)}) collective-permute-start(bf16[40,3072]{1,0:T(8,128)(2,1)S(1)} %shard_map.107), channel_id=1, source_target_pairs={{0,16},{1,3},{2,18},{3,1},{4,20},{5,7},{6,22},{7,5},{8,24},{9,11},... | collective-permute-start | bytes 737288 | tf_op jit(solution)/shard_map/ppermute | solution.py:281
  91.2 2.0 %collective-permute-start.36 = (bf16[40,3072]{1,0:T(8,128)(2,1)S(1)}, bf16[40,3072]{1,0:T(8,128)(2,1)S(1)}, u32[]{:S(2)}, u32[]{:S(2)}) collective-permute-start(bf16[40,3072]{1,0:T(8,128)(2,1)S(1)} %get-tuple-element.35), channel_id=1, source_target_pairs={{0,2},{1,3},{2,0},{3,1},{4,6},{5,7},{6,4},{7,5},{8,10},{9,11},{10,... | collective-permute-start | bytes 737288 | tf_op jit(solution)/shard_map/ppermute | solution.py:281
  93.8 5.0 %collective-permute-done.14.far_ref = bf16[40,3072]{1,0:T(8,128)(2,1)S(1)} collective-permute-done((bf16[40,3072]{1,0:T(8,128)(2,1)S(1)}, bf16[40,3072]{1,0:T(8,128)(2,1)S(1)}, u32[]{:S(2)}, u32[]{:S(2)}) %collective-permute-start.14) | collective-permute-done | bytes 245792 | tf_op jit(solution)/shard_map/ppermute | solution.py:281
  99.0 5.1 %collective-permute-done.5.far_ref = bf16[40,3072]{1,0:T(8,128)(2,1)S(1)} collective-permute-done((bf16[40,3072]{1,0:T(8,128)(2,1)S(1)}, bf16[40,3072]{1,0:T(8,128)(2,1)S(1)}, u32[]{:S(2)}, u32[]{:S(2)}) %collective-permute-start.5) | collective-permute-done | bytes 245792 | tf_op jit(solution)/shard_map/ppermute | solution.py:281
  104.1 5.3 %collective-permute-done.35.x_ref = bf16[40,3072]{1,0:T(8,128)(2,1)S(1)} collective-permute-done((bf16[40,3072]{1,0:T(8,128)(2,1)S(1)}, bf16[40,3072]{1,0:T(8,128)(2,1)S(1)}, u32[]{:S(2)}, u32[]{:S(2)}) %collective-permute-start.35) | collective-permute-done | bytes 245792 | tf_op jit(solution)/shard_map/ppermute | solution.py:281
  109.5 2.1 %collective-permute-start.6 = (bf16[40,3072]{1,0:T(8,128)(2,1)S(1)}, bf16[40,3072]{1,0:T(8,128)(2,1)S(1)}, u32[]{:S(2)}, u32[]{:S(2)}) collective-permute-start(bf16[40,3072]{1,0:T(8,128)(2,1)S(1)} %get-tuple-element.22), channel_id=1, source_target_pairs={{0,16},{1,17},{2,18},{3,19},{4,20},{5,21},{6,22},{7,23},{8,24},{9,... | collective-permute-start | bytes 737288 | tf_op jit(solution)/shard_map/ppermute | solution.py:281
  111.8 2.6 %collective-permute-done.25.x_ref = bf16[40,3072]{1,0:T(8,128)(2,1)S(1)} collective-permute-done((bf16[40,3072]{1,0:T(8,128)(2,1)S(1)}, bf16[40,3072]{1,0:T(8,128)(2,1)S(1)}, u32[]{:S(2)}, u32[]{:S(2)}) %collective-permute-start.25) | collective-permute-done | bytes 245792 | tf_op jit(solution)/shard_map/ppermute | solution.py:281
  114.4 4.9 %collective-permute-start.37 = (bf16[40,3072]{1,0:T(8,128)(2,1)S(1)}, bf16[40,3072]{1,0:T(8,128)(2,1)S(1)}, u32[]{:S(2)}, u32[]{:S(2)}) collective-permute-start(bf16[40,3072]{1,0:T(8,128)(2,1)S(1)} %shard_map.124), channel_id=1, source_target_pairs={{0,4},{1,5},{2,6},{3,7},{4,0},{5,1},{6,2},{7,3},{8,12},{9,13},{10,... | collective-permute-start | bytes 737288 | tf_op jit(solution)/shard_map/ppermute | solution.py:281
  120.2 3.5 %collective-permute-start.17 = (bf16[40,3072]{1,0:T(8,128)(2,1)S(1)}, bf16[40,3072]{1,0:T(8,128)(2,1)S(1)}, u32[]{:S(2)}, u32[]{:S(2)}) collective-permute-start(bf16[40,3072]{1,0:T(8,128)(2,1)S(1)} %shard_map.114), channel_id=1, source_target_pairs={{0,12},{1,13},{2,14},{3,15},{4,8},{5,9},{6,10},{7,11},{8,4},{9,5},... | collective-permute-start | bytes 737288 | tf_op jit(solution)/shard_map/ppermute | solution.py:281
  123.9 3.4 %collective-permute-done.37.refs_3_ = bf16[40,3072]{1,0:T(8,128)(2,1)S(1)} collective-permute-done((bf16[40,3072]{1,0:T(8,128)(2,1)S(1)}, bf16[40,3072]{1,0:T(8,128)(2,1)S(1)}, u32[]{:S(2)}, u32[]{:S(2)}) %collective-permute-start.37) | collective-permute-done | bytes 245792 | tf_op jit(solution)/shard_map/ppermute | solution.py:281
  127.3 7.3 %collective-permute-done.27.refs_2_ = bf16[40,3072]{1,0:T(8,128)(2,1)S(1)} collective-permute-done((bf16[40,3072]{1,0:T(8,128)(2,1)S(1)}, bf16[40,3072]{1,0:T(8,128)(2,1)S(1)}, u32[]{:S(2)}, u32[]{:S(2)}) %collective-permute-start.27) | collective-permute-done | bytes 245792 | tf_op jit(solution)/shard_map/ppermute | solution.py:281
  136.3 11.3 %all_to_all.6 = f32[16,1,8]{2,1,0:T(1,128)S(1)} all-to-all(f32[16,1,8]{2,1,0:T(1,128)S(1)} %broadcast_in_dim.20), channel_id=1, replica_groups=mesh['rep'=2,'mp'=16] {'mp'}, dimensions={0} | all-to-all | bytes 1024 | tf_op jit(solution)/shard_map/all_to_all | solution.py:336
  (103 shorter events, 43.0 us)
Async XLA Ops:
  2.4 9.1 %collective-permute-start.28 = (bf16[40,3072]{1,0:T(8,128)(2,1)S(1)}, bf16[40,3072]{1,0:T(8,128)(2,1)S(1)}, u32[]{:S(2)}, u32[]{:S(2)}) collective-permute-start(bf16[40,3072]{1,0:T(8,128)(2,1)S(1)} %shard_map.104.mine_ref), channel_id=1, source_target_pairs={{0,4},{1,5},{2,6},{3,7},{4,0},{5,1},{6,2},{7,3},{8,12},{9,13},{10,... | collective-permute-start | bytes 737288 | tf_op jit(solution)/shard_map/ppermute | solution.py:281
  14.7 12.4 %collective-permute-start.18 = (bf16[40,3072]{1,0:T(8,128)(2,1)S(1)}, bf16[40,3072]{1,0:T(8,128)(2,1)S(1)}, u32[]{:S(2)}, u32[]{:S(2)}) collective-permute-start(bf16[40,3072]{1,0:T(8,128)(2,1)S(1)} %shard_map.104.mine_ref), channel_id=1, source_target_pairs={{0,8},{1,9},{2,10},{3,11},{4,12},{5,13},{6,14},{7,15},{8,0},{9,1},... | collective-permute-start | bytes 737288 | tf_op jit(solution)/shard_map/ppermute | solution.py:281
  19.8 11.9 %collective-permute-start.31 = (bf16[40,3072]{1,0:T(8,128)(2,1)S(1)}, bf16[40,3072]{1,0:T(8,128)(2,1)S(1)}, u32[]{:S(2)}, u32[]{:S(2)}) collective-permute-start(bf16[40,3072]{1,0:T(8,128)(2,1)S(1)} %shard_map.120), channel_id=1, source_target_pairs={{0,16},{1,3},{2,18},{3,1},{4,20},{5,7},{6,22},{7,5},{8,24},{9,11},... | collective-permute-start | bytes 737288 | tf_op jit(solution)/shard_map/ppermute | solution.py:281
  31.7 31.0 %collective-permute-start.32 = (bf16[160,3072]{1,0:T(8,128)(2,1)S(1)}, bf16[160,3072]{1,0:T(8,128)(2,1)S(1)}, u32[]{:S(2)}, u32[]{:S(2)}) collective-permute-start(bf16[160,3072]{1,0:T(8,128)(2,1)S(1)} %shard_map.121.refs_0_), channel_id=1, source_target_pairs={{0,1},{1,0},{2,3},{3,2},{4,5},{5,4},{6,7},{7,6},{8,9},{9,8},{10,11... | collective-permute-start | bytes 2949128 | tf_op jit(solution)/shard_map/ppermute | solution.py:281
  41.4 26.2 %collective-permute-start.22 = (bf16[160,3072]{1,0:T(8,128)(2,1)S(1)}, bf16[160,3072]{1,0:T(8,128)(2,1)S(1)}, u32[]{:S(2)}, u32[]{:S(2)}) collective-permute-start(bf16[160,3072]{1,0:T(8,128)(2,1)S(1)} %shard_map.116.refs_0_), channel_id=1, source_target_pairs={{0,1},{1,0},{2,3},{3,2},{4,5},{5,4},{6,7},{7,6},{8,9},{9,8},{10,11... | collective-permute-start | bytes 2949128 | tf_op jit(solution)/shard_map/ppermute | solution.py:281
  41.5 9.6 %collective-permute-start = (bf16[40,3072]{1,0:T(8,128)(2,1)S(1)}, bf16[40,3072]{1,0:T(8,128)(2,1)S(1)}, u32[]{:S(2)}, u32[]{:S(2)}) collective-permute-start(bf16[40,3072]{1,0:T(8,128)(2,1)S(1)} %shard_map.104.mine_ref), channel_id=1, source_target_pairs={{0,16},{1,17},{2,18},{3,19},{4,20},{5,21},{6,22},{7,23},{8,24},{9,... | collective-permute-start | bytes 737288 | tf_op jit(solution)/shard_map/ppermute | solution.py:281
  52.5 9.6 %collective-permute-start.2 = (bf16[40,3072]{1,0:T(8,128)(2,1)S(1)}, bf16[40,3072]{1,0:T(8,128)(2,1)S(1)}, u32[]{:S(2)}, u32[]{:S(2)}) collective-permute-start(bf16[40,3072]{1,0:T(8,128)(2,1)S(1)} %shard_map.105), channel_id=1, source_target_pairs={{0,16},{1,3},{2,18},{3,1},{4,20},{5,7},{6,22},{7,5},{8,24},{9,11},... | collective-permute-start | bytes 737288 | tf_op jit(solution)/shard_map/ppermute | solution.py:281
  54.2 18.7 %collective-permute-start.12 = (bf16[160,3072]{1,0:T(8,128)(2,1)S(1)}, bf16[160,3072]{1,0:T(8,128)(2,1)}, u32[]{:S(2)}, u32[]{:S(2)}) collective-permute-start(bf16[160,3072]{1,0:T(8,128)(2,1)S(1)} %shard_map.111.refs_0_), channel_id=1, source_target_pairs={{0,1},{1,0},{2,3},{3,2},{4,5},{5,4},{6,7},{7,6},{8,9},{9,8},{10,11... | collective-permute-start | bytes 2949128 | tf_op jit(solution)/shard_map/ppermute | solution.py:281
  62.2 17.0 %collective-permute-start.3 = (bf16[160,3072]{1,0:T(8,128)(2,1)S(1)}, bf16[160,3072]{1,0:T(8,128)(2,1)S(1)}, u32[]{:S(2)}, u32[]{:S(2)}) collective-permute-start(bf16[160,3072]{1,0:T(8,128)(2,1)S(1)} %shard_map.106.refs_0_), channel_id=1, source_target_pairs={{0,1},{1,0},{2,3},{3,2},{4,5},{5,4},{6,7},{7,6},{8,9},{9,8},{10,11... | collective-permute-start | bytes 2949128 | tf_op jit(solution)/shard_map/ppermute | solution.py:281
  67.5 16.8 %collective-permute-start.33 = (bf16[160,3072]{1,0:T(8,128)(2,1)S(1)}, bf16[160,3072]{1,0:T(8,128)(2,1)S(1)}, u32[]{:S(2)}, u32[]{:S(2)}) collective-permute-start(bf16[160,3072]{1,0:T(8,128)(2,1)S(1)} %get-tuple-element.33), channel_id=1, source_target_pairs={{0,1},{1,0},{2,3},{3,2},{4,5},{5,4},{6,7},{7,6},{8,9},{9,8},{10,11... | collective-permute-start | bytes 2949128 | tf_op jit(solution)/shard_map/ppermute | solution.py:281
  72.6 11.9 %collective-permute-start.23 = (bf16[160,3072]{1,0:T(8,128)(2,1)S(1)}, bf16[160,3072]{1,0:T(8,128)(2,1)S(1)}, u32[]{:S(2)}, u32[]{:S(2)}) collective-permute-start(bf16[160,3072]{1,0:T(8,128)(2,1)S(1)} %get-tuple-element.29), channel_id=1, source_target_pairs={{0,1},{1,0},{2,3},{3,2},{4,5},{5,4},{6,7},{7,6},{8,9},{9,8},{10,11... | collective-permute-start | bytes 2949128 | tf_op jit(solution)/shard_map/ppermute | solution.py:281
  86.7 12.1 %collective-permute-start.14 = (bf16[40,3072]{1,0:T(8,128)(2,1)S(1)}, bf16[40,3072]{1,0:T(8,128)(2,1)S(1)}, u32[]{:S(2)}, u32[]{:S(2)}) collective-permute-start(bf16[40,3072]{1,0:T(8,128)(2,1)S(1)} %shard_map.112), channel_id=1, source_target_pairs={{0,16},{1,3},{2,18},{3,1},{4,20},{5,7},{6,22},{7,5},{8,24},{9,11},... | collective-permute-start | bytes 737288 | tf_op jit(solution)/shard_map/ppermute | solution.py:281
  86.9 17.2 %collective-permute-start.5 = (bf16[40,3072]{1,0:T(8,128)(2,1)S(1)}, bf16[40,3072]{1,0:T(8,128)(2,1)S(1)}, u32[]{:S(2)}, u32[]{:S(2)}) collective-permute-start(bf16[40,3072]{1,0:T(8,128)(2,1)S(1)} %shard_map.107), channel_id=1, source_target_pairs={{0,16},{1,3},{2,18},{3,1},{4,20},{5,7},{6,22},{7,5},{8,24},{9,11},... | collective-permute-start | bytes 737288 | tf_op jit(solution)/shard_map/ppermute | solution.py:281
  91.1 18.3 %collective-permute-start.35 = (bf16[40,3072]{1,0:T(8,128)(2,1)S(1)}, bf16[40,3072]{1,0:T(8,128)(2,1)S(1)}, u32[]{:S(2)}, u32[]{:S(2)}) collective-permute-start(bf16[40,3072]{1,0:T(8,128)(2,1)S(1)} %get-tuple-element.34), channel_id=1, source_target_pairs={{0,16},{1,17},{2,18},{3,19},{4,20},{5,21},{6,22},{7,23},{8,24},{9,... | collective-permute-start | bytes 737288 | tf_op jit(solution)/shard_map/ppermute | solution.py:281
  91.2 18.4 %collective-permute-start.36 = (bf16[40,3072]{1,0:T(8,128)(2,1)S(1)}, bf16[40,3072]{1,0:T(8,128)(2,1)S(1)}, u32[]{:S(2)}, u32[]{:S(2)}) collective-permute-start(bf16[40,3072]{1,0:T(8,128)(2,1)S(1)} %get-tuple-element.35), channel_id=1, source_target_pairs={{0,2},{1,3},{2,0},{3,1},{4,6},{5,7},{6,4},{7,5},{8,10},{9,11},{10,... | collective-permute-start | bytes 737288 | tf_op jit(solution)/shard_map/ppermute | solution.py:281
  93.7 20.7 %collective-permute-start.25 = (bf16[40,3072]{1,0:T(8,128)(2,1)S(1)}, bf16[40,3072]{1,0:T(8,128)(2,1)S(1)}, u32[]{:S(2)}, u32[]{:S(2)}) collective-permute-start(bf16[40,3072]{1,0:T(8,128)(2,1)S(1)} %get-tuple-element.30), channel_id=1, source_target_pairs={{0,16},{1,17},{2,18},{3,19},{4,20},{5,21},{6,22},{7,23},{8,24},{9,... | collective-permute-start | bytes 737288 | tf_op jit(solution)/shard_map/ppermute | solution.py:281
  98.8 15.6 %collective-permute-start.26 = (bf16[40,3072]{1,0:T(8,128)(2,1)S(1)}, bf16[40,3072]{1,0:T(8,128)(2,1)S(1)}, u32[]{:S(2)}, u32[]{:S(2)}) collective-permute-start(bf16[40,3072]{1,0:T(8,128)(2,1)S(1)} %get-tuple-element.31), channel_id=1, source_target_pairs={{0,2},{1,3},{2,0},{3,1},{4,6},{5,7},{6,4},{7,5},{8,10},{9,11},{10,... | collective-permute-start | bytes 737288 | tf_op jit(solution)/shard_map/ppermute | solution.py:281
  104.1 15.4 %collective-permute-start.15 = (bf16[40,3072]{1,0:T(8,128)(2,1)S(1)}, bf16[40,3072]{1,0:T(8,128)(2,1)S(1)}, u32[]{:S(2)}, u32[]{:S(2)}) collective-permute-start(bf16[40,3072]{1,0:T(8,128)(2,1)S(1)} %get-tuple-element.26), channel_id=1, source_target_pairs={{0,16},{1,17},{2,18},{3,19},{4,20},{5,21},{6,22},{7,23},{8,24},{9,... | collective-permute-start | bytes 737288 | tf_op jit(solution)/shard_map/ppermute | solution.py:281
  109.4 10.7 %collective-permute-start.16 = (bf16[40,3072]{1,0:T(8,128)(2,1)S(1)}, bf16[40,3072]{1,0:T(8,128)(2,1)S(1)}, u32[]{:S(2)}, u32[]{:S(2)}) collective-permute-start(bf16[40,3072]{1,0:T(8,128)(2,1)S(1)} %get-tuple-element.27), channel_id=1, source_target_pairs={{0,2},{1,3},{2,0},{3,1},{4,6},{5,7},{6,4},{7,5},{8,10},{9,11},{10,... | collective-permute-start | bytes 737288 | tf_op jit(solution)/shard_map/ppermute | solution.py:281
  109.5 14.2 %collective-permute-start.6 = (bf16[40,3072]{1,0:T(8,128)(2,1)S(1)}, bf16[40,3072]{1,0:T(8,128)(2,1)S(1)}, u32[]{:S(2)}, u32[]{:S(2)}) collective-permute-start(bf16[40,3072]{1,0:T(8,128)(2,1)S(1)} %get-tuple-element.22), channel_id=1, source_target_pairs={{0,16},{1,17},{2,18},{3,19},{4,20},{5,21},{6,22},{7,23},{8,24},{9,... | collective-permute-start | bytes 737288 | tf_op jit(solution)/shard_map/ppermute | solution.py:281
  114.4 9.3 %collective-permute-start.7 = (bf16[40,3072]{1,0:T(8,128)(2,1)S(1)}, bf16[40,3072]{1,0:T(8,128)(2,1)S(1)}, u32[]{:S(2)}, u32[]{:S(2)}) collective-permute-start(bf16[40,3072]{1,0:T(8,128)(2,1)S(1)} %get-tuple-element.23), channel_id=1, source_target_pairs={{0,2},{1,3},{2,0},{3,1},{4,6},{5,7},{6,4},{7,5},{8,10},{9,11},{10,... | collective-permute-start | bytes 737288 | tf_op jit(solution)/shard_map/ppermute | solution.py:281
  114.4 12.8 %collective-permute-start.37 = (bf16[40,3072]{1,0:T(8,128)(2,1)S(1)}, bf16[40,3072]{1,0:T(8,128)(2,1)S(1)}, u32[]{:S(2)}, u32[]{:S(2)}) collective-permute-start(bf16[40,3072]{1,0:T(8,128)(2,1)S(1)} %shard_map.124), channel_id=1, source_target_pairs={{0,4},{1,5},{2,6},{3,7},{4,0},{5,1},{6,2},{7,3},{8,12},{9,13},{10,... | collective-permute-start | bytes 737288 | tf_op jit(solution)/shard_map/ppermute | solution.py:281
  119.5 15.1 %collective-permute-start.27 = (bf16[40,3072]{1,0:T(8,128)(2,1)S(1)}, bf16[40,3072]{1,0:T(8,128)(2,1)S(1)}, u32[]{:S(2)}, u32[]{:S(2)}) collective-permute-start(bf16[40,3072]{1,0:T(8,128)(2,1)S(1)} %shard_map.119), channel_id=1, source_target_pairs={{0,8},{1,9},{2,10},{3,11},{4,12},{5,13},{6,14},{7,15},{8,0},{9,1},... | collective-permute-start | bytes 737288 | tf_op jit(solution)/shard_map/ppermute | solution.py:281
  120.2 14.3 %collective-permute-start.17 = (bf16[40,3072]{1,0:T(8,128)(2,1)S(1)}, bf16[40,3072]{1,0:T(8,128)(2,1)S(1)}, u32[]{:S(2)}, u32[]{:S(2)}) collective-permute-start(bf16[40,3072]{1,0:T(8,128)(2,1)S(1)} %shard_map.114), channel_id=1, source_target_pairs={{0,12},{1,13},{2,14},{3,15},{4,8},{5,9},{6,10},{7,11},{8,4},{9,5},... | collective-permute-start | bytes 737288 | tf_op jit(solution)/shard_map/ppermute | solution.py:281
  (22 other events, 209.3 us)

commit v2 on v1

--- a/solution.py
+++ b/solution.py
@@ -138,6 +138,19 @@
         out_ref[...] = x_ref[...]
 
 
+def join_kernel(middle_ref, end_ref, out_ref):
+    place = lax.axis_index("mp") // 4
+    middle = (place == 1) | (place == 2)
+
+    @pl.when(middle)
+    def _():
+        out_ref[...] = middle_ref[...]
+
+    @pl.when(jnp.logical_not(middle))
+    def _():
+        out_ref[...] = end_ref[...]
+
+
 def stack_kernel(mine_ref, x_ref, y_ref, far_ref, out_ref):
     size = mine_ref.shape[0]
     for place, ref in enumerate((mine_ref, x_ref, y_ref, far_ref)):
@@ -276,8 +289,9 @@
         moves = []
         for rep in range(2):
             for mp in range(n_mp):
-                to_rep, to_mp = target(rep, mp)
-                moves.append((rep * n_mp + mp, to_rep * n_mp + to_mp))
+                to = target(rep, mp)
+                if to is not None:
+                    moves.append((rep * n_mp + mp, to[0] * n_mp + to[1]))
         return lax.ppermute(value, AXES, moves)
 
     def to_core(value):
@@ -306,8 +320,24 @@
 
     order = [0] + list(range(depth - 1, 0, -1))
     arrived = {0: normed}
-    for step in order[1:]:
-        arrived[step] = to_depth(normed, step)
+    if depth == 4:
+        arrived[1] = to_depth(normed, 1)
+
+        def swap_middle(value):
+            return permute(value, lambda rep, mp: (rep, mp ^ 12) if mp // 4 in (1, 2) else None)
+
+        def to_ends(value):
+            return permute(value, lambda rep, mp: (rep, mp ^ 4) if mp // 4 in (1, 2) else None)
+
+        middle = swap_middle(normed)
+        across = swap_middle(arrived[1])
+        passed = to_ends(middle)
+        arrived[2] = local(join_kernel, (across, passed), [(size, width)])
+        passed = to_ends(across)
+        arrived[3] = local(join_kernel, (middle, passed), [(size, width)])
+    else:
+        for step in order[1:]:
+            arrived[step] = to_depth(normed, step)
     sums = {}
     for step in order:
         mine = arrived[step]

time: 149 us -> 143 us (0.960)
  starting transfers between devices: 44.6 us -> 37.9 us
  waiting for transfers between devices: 57.1 us -> 58.7 us
    ppermute x38 -> x40, starting transfers between devices: 44.6 us -> 37.9 us  [permute(): return lax.ppermute(value, AXES, moves)]
    ppermute x38 -> x40, waiting for transfers between devices: 57.1 us -> 58.7 us  [permute(): return lax.ppermute(value, AXES, moves)]
  transfers between devices with their start and end apart: 38 -> 40, of which waited for: 20 -> 19; matrix products, arithmetic and copies ran while one was open for 0% -> 0% of each run, Pallas kernels for 20% -> 21%
where the time goes in v2:
time: 143 us
  waiting for transfers between devices  58.7 us (41%)
  starting transfers between devices  37.9 us (27%)
  Pallas kernels  31.2 us (22%)
  blocking collectives  10.8 us (8%)
  local copies, waits for them, and re-layouts  1.81 us (1%)
  between operations  1.71 us (1%)
    ppermute x40, waiting for transfers between devices, permute(): return lax.ppermute(value, AXES, moves)  58.7 us
    ppermute x40, starting transfers between devices, permute(): return lax.ppermute(value, AXES, moves)  37.9 us
    pallas_call x4, Pallas kernels, window(): pl.pallas_call(functools.partial(window_kernel, count, tile), out_shape=[...  20.5 us
    all_to_all x1, blocking collectives, tokens_travel(): totals = jnp.sum(lax.all_to_all(shares, 'mp', 0, 0, tiled=True), axis=0)  10.8 us
    pallas_call x4, Pallas kernels, relay(): pl.pallas_call(functools.partial(relay_kernel, start), out_shape=jax.Shap...  7.11 us
  transfers between devices with their start and end apart: 40, of which 19 were waited for; matrix products, arithmetic and copies ran while one was open for 0% of the time, Pallas kernels for 21%

profile of v2, /device:TPU:0, one launch (start us, length us, event | category | flops | bytes accessed | tf_op | source)
XLA Modules:
  0.0 142.8 jit_solution(5120446956568538295)
XLA Ops:
  2.4 3.1 %collective-permute-start.9 = (bf16[40,3072]{1,0:T(8,128)(2,1)S(1)}, bf16[40,3072]{1,0:T(8,128)(2,1)S(1)}, u32[]{:S(2)}, u32[]{:S(2)}) collective-permute-start(bf16[40,3072]{1,0:T(8,128)(2,1)S(1)} %shard_map.104.mine_ref), channel_id=1, source_target_pairs={{0,4},{1,5},{2,6},{3,7},{4,0},{5,1},{6,2},{7,3},{8,12},{9,13},{10,... | collective-permute-start | bytes 737288 | tf_op jit(solution)/shard_map/ppermute | solution.py:295
  6.2 5.3 %collective-permute-done.9.mine_ref = bf16[40,3072]{1,0:T(8,128)(2,1)S(1)} collective-permute-done((bf16[40,3072]{1,0:T(8,128)(2,1)S(1)}, bf16[40,3072]{1,0:T(8,128)(2,1)S(1)}, u32[]{:S(2)}, u32[]{:S(2)}) %collective-permute-start.9) | collective-permute-done | bytes 245792 | tf_op jit(solution)/shard_map/ppermute | solution.py:295
  16.7 2.0 %collective-permute-done.31.x_ref = bf16[40,3072]{1,0:T(8,128)(2,1)S(1)} collective-permute-done((bf16[40,3072]{1,0:T(8,128)(2,1)S(1)}, bf16[40,3072]{1,0:T(8,128)(2,1)S(1)}, u32[]{:S(2)}, u32[]{:S(2)}) %collective-permute-start.31) | collective-permute-done | bytes 245792 | tf_op jit(solution)/shard_map/ppermute | solution.py:295
  20.5 4.8 %collective-permute-done.21.end_ref = bf16[40,3072]{1,0:T(8,128)(2,1)S(1)} collective-permute-done((bf16[40,3072]{1,0:T(8,128)(2,1)S(1)}, bf16[40,3072]{1,0:T(8,128)(2,1)S(1)}, u32[]{:S(2)}, u32[]{:S(2)}) %collective-permute-start.21) | collective-permute-done | bytes 245792 | tf_op jit(solution)/shard_map/ppermute | solution.py:295
  27.9 3.7 %collective-permute-done.22.x_ref = bf16[40,3072]{1,0:T(8,128)(2,1)S(1)} collective-permute-done((bf16[40,3072]{1,0:T(8,128)(2,1)S(1)}, bf16[40,3072]{1,0:T(8,128)(2,1)S(1)}, u32[]{:S(2)}, u32[]{:S(2)}) %collective-permute-start.22) | collective-permute-done | bytes 245792 | tf_op jit(solution)/shard_map/ppermute | solution.py:295
  32.3 2.3 %collective-permute-start.24 = (bf16[40,3072]{1,0:T(8,128)(2,1)S(1)}, bf16[40,3072]{1,0:T(8,128)(2,1)S(1)}, u32[]{:S(2)}, u32[]{:S(2)}) collective-permute-start(bf16[40,3072]{1,0:T(8,128)(2,1)S(1)} %shard_map.117), channel_id=1, source_target_pairs={{0,16},{1,3},{2,18},{3,1},{4,20},{5,7},{6,22},{7,5},{8,24},{9,11},... | collective-permute-start | bytes 737288 | tf_op jit(solution)/shard_map/ppermute | solution.py:295
  38.9 2.1 %collective-permute-start = (bf16[40,3072]{1,0:T(8,128)(2,1)S(1)}, bf16[40,3072]{1,0:T(8,128)(2,1)S(1)}, u32[]{:S(2)}, u32[]{:S(2)}) collective-permute-start(bf16[40,3072]{1,0:T(8,128)(2,1)S(1)} %shard_map.104.mine_ref), channel_id=1, source_target_pairs={{0,16},{1,17},{2,18},{3,19},{4,20},{5,21},{6,22},{7,23},{8,24},{9,... | collective-permute-start | bytes 737288 | tf_op jit(solution)/shard_map/ppermute | solution.py:295
  44.3 3.2 %collective-permute-done.x_ref = bf16[40,3072]{1,0:T(8,128)(2,1)S(1)} collective-permute-done((bf16[40,3072]{1,0:T(8,128)(2,1)S(1)}, bf16[40,3072]{1,0:T(8,128)(2,1)S(1)}, u32[]{:S(2)}, u32[]{:S(2)}) %collective-permute-start) | collective-permute-done | bytes 245792 | tf_op jit(solution)/shard_map/ppermute | solution.py:295
  47.5 2.7 %collective-permute-done.1.y_ref = bf16[40,3072]{1,0:T(8,128)(2,1)S(1)} collective-permute-done((bf16[40,3072]{1,0:T(8,128)(2,1)S(1)}, bf16[40,3072]{1,0:T(8,128)(2,1)S(1)}, u32[]{:S(2)}, u32[]{:S(2)}) %collective-permute-start.1) | collective-permute-done | bytes 245792 | tf_op jit(solution)/shard_map/ppermute | solution.py:295
  50.3 2.1 %collective-permute-start.2 = (bf16[40,3072]{1,0:T(8,128)(2,1)S(1)}, bf16[40,3072]{1,0:T(8,128)(2,1)S(1)}, u32[]{:S(2)}, u32[]{:S(2)}) collective-permute-start(bf16[40,3072]{1,0:T(8,128)(2,1)S(1)} %shard_map.105), channel_id=1, source_target_pairs={{0,16},{1,3},{2,18},{3,1},{4,20},{5,7},{6,22},{7,5},{8,24},{9,11},... | collective-permute-start | bytes 737288 | tf_op jit(solution)/shard_map/ppermute | solution.py:295
  60.9 4.8 %window.7 = (bf16[160,3072]{1,0:T(8,128)(2,1)S(1)}, bf16[160,3072]{1,0:T(8,128)(2,1)S(1)}) custom-call(s32[1]{0:T(128)S(6)} %copy.13.owner_ref, bf16[160,3072]{1,0:T(8,128)(2,1)S(1)} %shard_map.123.refs_0_, bf16[160,3072]{1,0:T(8,128)(2,1)S(1)} %collective-permute-done.34.refs_1_, bf16[768,1536]{1,0:T(8,128)(2,1)S(1)} %relay.4.refs_2_, ...), custom_call_target="tpu_custom_call" | custom-call | flops 4529848320 | bytes 3932160 | tf_op jit(solution)/shard_map/window/pallas_call | solution.py:87
  65.8 5.0 %window.6 = (bf16[160,3072]{1,0:T(8,128)(2,1)S(1)}, bf16[160,3072]{1,0:T(8,128)(2,1)S(1)}) custom-call(s32[1]{0:T(128)S(6)} %copy.13.owner_ref, bf16[160,3072]{1,0:T(8,128)(2,1)S(1)} %shard_map.118.refs_0_, bf16[160,3072]{1,0:T(8,128)(2,1)S(1)} %collective-permute-done.25.refs_1_, bf16[768,1536]{1,0:T(8,128)(2,1)S(1)} %relay.4.refs_2_, ...), custom_call_target="tpu_custom_call" | custom-call | flops 4529848320 | bytes 3932160 | tf_op jit(solution)/shard_map/window/pallas_call | solution.py:87
  71.1 6.0 %window.5 = (bf16[160,3072]{1,0:T(8,128)(2,1)S(1)}, bf16[160,3072]{1,0:T(8,128)(2,1)S(1)}) custom-call(s32[1]{0:T(128)S(6)} %copy.13.owner_ref, bf16[160,3072]{1,0:T(8,128)(2,1)S(1)} %shard_map.112.refs_0_, bf16[160,3072]{1,0:T(8,128)(2,1)} %collective-permute-done.15.refs_1_, bf16[768,1536]{1,0:T(8,128)(2,1)S(1)} %relay.4.refs_2_, ...), custom_call_target="tpu_custom_call" | custom-call | flops 4529848320 | bytes 3932160 | tf_op jit(solution)/shard_map/window/pallas_call | solution.py:87
  77.4 4.8 %window.4 = (bf16[160,3072]{1,0:T(8,128)(2,1)S(1)}, bf16[160,3072]{1,0:T(8,128)(2,1)S(1)}) custom-call(s32[1]{0:T(128)S(6)} %copy.13.owner_ref, bf16[160,3072]{1,0:T(8,128)(2,1)S(1)} %shard_map.106.refs_0_, bf16[160,3072]{1,0:T(8,128)(2,1)S(1)} %collective-permute-done.3.refs_1_, bf16[768,1536]{1,0:T(8,128)(2,1)S(1)} %relay.4.refs_2_, ...), custom_call_target="tpu_custom_call" | custom-call | flops 4529848320 | bytes 3932160 | tf_op jit(solution)/shard_map/window/pallas_call | solution.py:87
  82.8 2.1 %collective-permute-start.27 = (bf16[40,3072]{1,0:T(8,128)(2,1)S(1)}, bf16[40,3072]{1,0:T(8,128)(2,1)S(1)}, u32[]{:S(2)}, u32[]{:S(2)}) collective-permute-start(bf16[40,3072]{1,0:T(8,128)(2,1)S(1)} %shard_map.119), channel_id=1, source_target_pairs={{0,16},{1,3},{2,18},{3,1},{4,20},{5,7},{6,22},{7,5},{8,24},{9,11},... | collective-permute-start | bytes 737288 | tf_op jit(solution)/shard_map/ppermute | solution.py:295
  85.1 2.1 %collective-permute-start.5 = (bf16[40,3072]{1,0:T(8,128)(2,1)S(1)}, bf16[40,3072]{1,0:T(8,128)(2,1)S(1)}, u32[]{:S(2)}, u32[]{:S(2)}) collective-permute-start(bf16[40,3072]{1,0:T(8,128)(2,1)S(1)} %shard_map.107), channel_id=1, source_target_pairs={{0,16},{1,3},{2,18},{3,1},{4,20},{5,7},{6,22},{7,5},{8,24},{9,11},... | collective-permute-start | bytes 737288 | tf_op jit(solution)/shard_map/ppermute | solution.py:295
  92.0 5.0 %collective-permute-done.17.far_ref = bf16[40,3072]{1,0:T(8,128)(2,1)S(1)} collective-permute-done((bf16[40,3072]{1,0:T(8,128)(2,1)S(1)}, bf16[40,3072]{1,0:T(8,128)(2,1)S(1)}, u32[]{:S(2)}, u32[]{:S(2)}) %collective-permute-start.17) | collective-permute-done | bytes 245792 | tf_op jit(solution)/shard_map/ppermute | solution.py:295
  97.2 5.1 %collective-permute-done.5.far_ref = bf16[40,3072]{1,0:T(8,128)(2,1)S(1)} collective-permute-done((bf16[40,3072]{1,0:T(8,128)(2,1)S(1)}, bf16[40,3072]{1,0:T(8,128)(2,1)S(1)}, u32[]{:S(2)}, u32[]{:S(2)}) %collective-permute-start.5) | collective-permute-done | bytes 245792 | tf_op jit(solution)/shard_map/ppermute | solution.py:295
  102.3 5.3 %collective-permute-done.37.x_ref = bf16[40,3072]{1,0:T(8,128)(2,1)S(1)} collective-permute-done((bf16[40,3072]{1,0:T(8,128)(2,1)S(1)}, bf16[40,3072]{1,0:T(8,128)(2,1)S(1)}, u32[]{:S(2)}, u32[]{:S(2)}) %collective-permute-start.37) | collective-permute-done | bytes 245792 | tf_op jit(solution)/shard_map/ppermute | solution.py:295
  109.3 3.3 %collective-permute-done.28.x_ref = bf16[40,3072]{1,0:T(8,128)(2,1)S(1)} collective-permute-done((bf16[40,3072]{1,0:T(8,128)(2,1)S(1)}, bf16[40,3072]{1,0:T(8,128)(2,1)S(1)}, u32[]{:S(2)}, u32[]{:S(2)}) %collective-permute-start.28) | collective-permute-done | bytes 245792 | tf_op jit(solution)/shard_map/ppermute | solution.py:295
  116.1 2.7 %collective-permute-start.20 = (bf16[40,3072]{1,0:T(8,128)(2,1)S(1)}, bf16[40,3072]{1,0:T(8,128)(2,1)S(1)}, u32[]{:S(2)}, u32[]{:S(2)}) collective-permute-start(bf16[40,3072]{1,0:T(8,128)(2,1)S(1)} %shard_map.115), channel_id=1, source_target_pairs={{0,12},{1,13},{2,14},{3,15},{4,8},{5,9},{6,10},{7,11},{8,4},{9,5},... | collective-permute-start | bytes 737288 | tf_op jit(solution)/shard_map/ppermute | solution.py:295
  118.9 3.1 %collective-permute-done.39.refs_3_ = bf16[40,3072]{1,0:T(8,128)(2,1)S(1)} collective-permute-done((bf16[40,3072]{1,0:T(8,128)(2,1)S(1)}, bf16[40,3072]{1,0:T(8,128)(2,1)S(1)}, u32[]{:S(2)}, u32[]{:S(2)}) %collective-permute-start.39) | collective-permute-done | bytes 245792 | tf_op jit(solution)/shard_map/ppermute | solution.py:295
  122.0 7.7 %collective-permute-done.30.refs_2_ = bf16[40,3072]{1,0:T(8,128)(2,1)S(1)} collective-permute-done((bf16[40,3072]{1,0:T(8,128)(2,1)S(1)}, bf16[40,3072]{1,0:T(8,128)(2,1)S(1)}, u32[]{:S(2)}, u32[]{:S(2)}) %collective-permute-start.30) | collective-permute-done | bytes 245792 | tf_op jit(solution)/shard_map/ppermute | solution.py:295
  131.4 10.8 %all_to_all.6 = f32[16,1,8]{2,1,0:T(1,128)S(1)} all-to-all(f32[16,1,8]{2,1,0:T(1,128)S(1)} %broadcast_in_dim.20), channel_id=1, replica_groups=mesh['rep'=2,'mp'=16] {'mp'}, dimensions={0} | all-to-all | bytes 1024 | tf_op jit(solution)/shard_map/all_to_all | solution.py:366
  (109 shorter events, 42.3 us)
Async XLA Ops:
  2.4 9.1 %collective-permute-start.9 = (bf16[40,3072]{1,0:T(8,128)(2,1)S(1)}, bf16[40,3072]{1,0:T(8,128)(2,1)S(1)}, u32[]{:S(2)}, u32[]{:S(2)}) collective-permute-start(bf16[40,3072]{1,0:T(8,128)(2,1)S(1)} %shard_map.104.mine_ref), channel_id=1, source_target_pairs={{0,4},{1,5},{2,6},{3,7},{4,0},{5,1},{6,2},{7,3},{8,12},{9,13},{10,... | collective-permute-start | bytes 737288 | tf_op jit(solution)/shard_map/ppermute | solution.py:295
  5.6 9.8 %collective-permute-start.8 = (bf16[40,3072]{1,0:T(8,128)(2,1)S(1)}, bf16[40,3072]{1,0:T(8,128)(2,1)S(1)}, u32[]{:S(2)}, u32[]{:S(2)}) collective-permute-start(bf16[40,3072]{1,0:T(8,128)(2,1)S(1)} %shard_map.104.mine_ref), channel_id=1, source_target_pairs={{4,8},{5,9},{6,10},{7,11},{8,4},{9,5},{10,6},{11,7},{20,24},{21,25... | collective-permute-start | bytes 737288 | tf_op jit(solution)/shard_map/ppermute | solution.py:295
  15.4 9.9 %collective-permute-start.21 = (bf16[40,3072]{1,0:T(8,128)(2,1)S(1)}, bf16[40,3072]{1,0:T(8,128)(2,1)S(1)}, u32[]{:S(2)}, u32[]{:S(2)}) collective-permute-start(bf16[40,3072]{1,0:T(8,128)(2,1)S(1)} %collective-permute-done.8.middle_ref), channel_id=1, source_target_pairs={{4,0},{5,1},{6,2},{7,3},{8,12},{9,13},{10,14},{11,15},{20,16},{21,... | collective-permute-start | bytes 737288 | tf_op jit(solution)/shard_map/ppermute | solution.py:295
  27.8 33.1 %collective-permute-start.34 = (bf16[160,3072]{1,0:T(8,128)(2,1)S(1)}, bf16[160,3072]{1,0:T(8,128)(2,1)S(1)}, u32[]{:S(2)}, u32[]{:S(2)}) collective-permute-start(bf16[160,3072]{1,0:T(8,128)(2,1)S(1)} %shard_map.123.refs_0_), channel_id=1, source_target_pairs={{0,1},{1,0},{2,3},{3,2},{4,5},{5,4},{6,7},{7,6},{8,9},{9,8},{10,11... | collective-permute-start | bytes 2949128 | tf_op jit(solution)/shard_map/ppermute | solution.py:295
  38.8 27.0 %collective-permute-start.25 = (bf16[160,3072]{1,0:T(8,128)(2,1)S(1)}, bf16[160,3072]{1,0:T(8,128)(2,1)S(1)}, u32[]{:S(2)}, u32[]{:S(2)}) collective-permute-start(bf16[160,3072]{1,0:T(8,128)(2,1)S(1)} %shard_map.118.refs_0_), channel_id=1, source_target_pairs={{0,1},{1,0},{2,3},{3,2},{4,5},{5,4},{6,7},{7,6},{8,9},{9,8},{10,11... | collective-permute-start | bytes 2949128 | tf_op jit(solution)/shard_map/ppermute | solution.py:295
  41.4 8.8 %collective-permute-start.1 = (bf16[40,3072]{1,0:T(8,128)(2,1)S(1)}, bf16[40,3072]{1,0:T(8,128)(2,1)S(1)}, u32[]{:S(2)}, u32[]{:S(2)}) collective-permute-start(bf16[40,3072]{1,0:T(8,128)(2,1)S(1)} %shard_map.104.mine_ref), channel_id=1, source_target_pairs={{0,2},{1,3},{2,0},{3,1},{4,6},{5,7},{6,4},{7,5},{8,10},{9,11},{10,... | collective-permute-start | bytes 737288 | tf_op jit(solution)/shard_map/ppermute | solution.py:295
  42.8 9.6 %collective-permute-start.14 = (bf16[40,3072]{1,0:T(8,128)(2,1)S(1)}, bf16[40,3072]{1,0:T(8,128)(2,1)S(1)}, u32[]{:S(2)}, u32[]{:S(2)}) collective-permute-start(bf16[40,3072]{1,0:T(8,128)(2,1)S(1)} %shard_map.111), channel_id=1, source_target_pairs={{0,16},{1,3},{2,18},{3,1},{4,20},{5,7},{6,22},{7,5},{8,24},{9,11},... | collective-permute-start | bytes 737288 | tf_op jit(solution)/shard_map/ppermute | solution.py:295
  50.3 10.0 %collective-permute-start.2 = (bf16[40,3072]{1,0:T(8,128)(2,1)S(1)}, bf16[40,3072]{1,0:T(8,128)(2,1)S(1)}, u32[]{:S(2)}, u32[]{:S(2)}) collective-permute-start(bf16[40,3072]{1,0:T(8,128)(2,1)S(1)} %shard_map.105), channel_id=1, source_target_pairs={{0,16},{1,3},{2,18},{3,1},{4,20},{5,7},{6,22},{7,5},{8,24},{9,11},... | collective-permute-start | bytes 737288 | tf_op jit(solution)/shard_map/ppermute | solution.py:295
  52.4 18.7 %collective-permute-start.15 = (bf16[160,3072]{1,0:T(8,128)(2,1)S(1)}, bf16[160,3072]{1,0:T(8,128)(2,1)}, u32[]{:S(2)}, u32[]{:S(2)}) collective-permute-start(bf16[160,3072]{1,0:T(8,128)(2,1)S(1)} %shard_map.112.refs_0_), channel_id=1, source_target_pairs={{0,1},{1,0},{2,3},{3,2},{4,5},{5,4},{6,7},{7,6},{8,9},{9,8},{10,11... | collective-permute-start | bytes 2949128 | tf_op jit(solution)/shard_map/ppermute | solution.py:295
  60.4 17.0 %collective-permute-start.3 = (bf16[160,3072]{1,0:T(8,128)(2,1)S(1)}, bf16[160,3072]{1,0:T(8,128)(2,1)S(1)}, u32[]{:S(2)}, u32[]{:S(2)}) collective-permute-start(bf16[160,3072]{1,0:T(8,128)(2,1)S(1)} %shard_map.106.refs_0_), channel_id=1, source_target_pairs={{0,1},{1,0},{2,3},{3,2},{4,5},{5,4},{6,7},{7,6},{8,9},{9,8},{10,11... | collective-permute-start | bytes 2949128 | tf_op jit(solution)/shard_map/ppermute | solution.py:295
  65.7 16.8 %collective-permute-start.35 = (bf16[160,3072]{1,0:T(8,128)(2,1)S(1)}, bf16[160,3072]{1,0:T(8,128)(2,1)S(1)}, u32[]{:S(2)}, u32[]{:S(2)}) collective-permute-start(bf16[160,3072]{1,0:T(8,128)(2,1)S(1)} %get-tuple-element.33), channel_id=1, source_target_pairs={{0,1},{1,0},{2,3},{3,2},{4,5},{5,4},{6,7},{7,6},{8,9},{9,8},{10,11... | collective-permute-start | bytes 2949128 | tf_op jit(solution)/shard_map/ppermute | solution.py:295
  70.8 11.9 %collective-permute-start.26 = (bf16[160,3072]{1,0:T(8,128)(2,1)S(1)}, bf16[160,3072]{1,0:T(8,128)(2,1)S(1)}, u32[]{:S(2)}, u32[]{:S(2)}) collective-permute-start(bf16[160,3072]{1,0:T(8,128)(2,1)S(1)} %get-tuple-element.29), channel_id=1, source_target_pairs={{0,1},{1,0},{2,3},{3,2},{4,5},{5,4},{6,7},{7,6},{8,9},{9,8},{10,11... | collective-permute-start | bytes 2949128 | tf_op jit(solution)/shard_map/ppermute | solution.py:295
  82.8 9.0 %collective-permute-start.27 = (bf16[40,3072]{1,0:T(8,128)(2,1)S(1)}, bf16[40,3072]{1,0:T(8,128)(2,1)S(1)}, u32[]{:S(2)}, u32[]{:S(2)}) collective-permute-start(bf16[40,3072]{1,0:T(8,128)(2,1)S(1)} %shard_map.119), channel_id=1, source_target_pairs={{0,16},{1,3},{2,18},{3,1},{4,20},{5,7},{6,22},{7,5},{8,24},{9,11},... | collective-permute-start | bytes 737288 | tf_op jit(solution)/shard_map/ppermute | solution.py:295
  84.9 12.1 %collective-permute-start.17 = (bf16[40,3072]{1,0:T(8,128)(2,1)S(1)}, bf16[40,3072]{1,0:T(8,128)(2,1)S(1)}, u32[]{:S(2)}, u32[]{:S(2)}) collective-permute-start(bf16[40,3072]{1,0:T(8,128)(2,1)S(1)} %shard_map.113), channel_id=1, source_target_pairs={{0,16},{1,3},{2,18},{3,1},{4,20},{5,7},{6,22},{7,5},{8,24},{9,11},... | collective-permute-start | bytes 737288 | tf_op jit(solution)/shard_map/ppermute | solution.py:295
  85.1 17.2 %collective-permute-start.5 = (bf16[40,3072]{1,0:T(8,128)(2,1)S(1)}, bf16[40,3072]{1,0:T(8,128)(2,1)S(1)}, u32[]{:S(2)}, u32[]{:S(2)}) collective-permute-start(bf16[40,3072]{1,0:T(8,128)(2,1)S(1)} %shard_map.107), channel_id=1, source_target_pairs={{0,16},{1,3},{2,18},{3,1},{4,20},{5,7},{6,22},{7,5},{8,24},{9,11},... | collective-permute-start | bytes 737288 | tf_op jit(solution)/shard_map/ppermute | solution.py:295
  89.3 18.3 %collective-permute-start.37 = (bf16[40,3072]{1,0:T(8,128)(2,1)S(1)}, bf16[40,3072]{1,0:T(8,128)(2,1)S(1)}, u32[]{:S(2)}, u32[]{:S(2)}) collective-permute-start(bf16[40,3072]{1,0:T(8,128)(2,1)S(1)} %get-tuple-element.34), channel_id=1, source_target_pairs={{0,16},{1,17},{2,18},{3,19},{4,20},{5,21},{6,22},{7,23},{8,24},{9,... | collective-permute-start | bytes 737288 | tf_op jit(solution)/shard_map/ppermute | solution.py:295
  89.3 18.4 %collective-permute-start.38 = (bf16[40,3072]{1,0:T(8,128)(2,1)S(1)}, bf16[40,3072]{1,0:T(8,128)(2,1)S(1)}, u32[]{:S(2)}, u32[]{:S(2)}) collective-permute-start(bf16[40,3072]{1,0:T(8,128)(2,1)S(1)} %get-tuple-element.35), channel_id=1, source_target_pairs={{0,2},{1,3},{2,0},{3,1},{4,6},{5,7},{6,4},{7,5},{8,10},{9,11},{10,... | collective-permute-start | bytes 737288 | tf_op jit(solution)/shard_map/ppermute | solution.py:295
  91.9 20.7 %collective-permute-start.28 = (bf16[40,3072]{1,0:T(8,128)(2,1)S(1)}, bf16[40,3072]{1,0:T(8,128)(2,1)S(1)}, u32[]{:S(2)}, u32[]{:S(2)}) collective-permute-start(bf16[40,3072]{1,0:T(8,128)(2,1)S(1)} %get-tuple-element.30), channel_id=1, source_target_pairs={{0,16},{1,17},{2,18},{3,19},{4,20},{5,21},{6,22},{7,23},{8,24},{9,... | collective-permute-start | bytes 737288 | tf_op jit(solution)/shard_map/ppermute | solution.py:295
  97.0 15.6 %collective-permute-start.29 = (bf16[40,3072]{1,0:T(8,128)(2,1)S(1)}, bf16[40,3072]{1,0:T(8,128)(2,1)S(1)}, u32[]{:S(2)}, u32[]{:S(2)}) collective-permute-start(bf16[40,3072]{1,0:T(8,128)(2,1)S(1)} %get-tuple-element.31), channel_id=1, source_target_pairs={{0,2},{1,3},{2,0},{3,1},{4,6},{5,7},{6,4},{7,5},{8,10},{9,11},{10,... | collective-permute-start | bytes 737288 | tf_op jit(solution)/shard_map/ppermute | solution.py:295
  102.3 12.9 %collective-permute-start.18 = (bf16[40,3072]{1,0:T(8,128)(2,1)S(1)}, bf16[40,3072]{1,0:T(8,128)(2,1)S(1)}, u32[]{:S(2)}, u32[]{:S(2)}) collective-permute-start(bf16[40,3072]{1,0:T(8,128)(2,1)S(1)} %get-tuple-element.26), channel_id=1, source_target_pairs={{0,16},{1,17},{2,18},{3,19},{4,20},{5,21},{6,22},{7,23},{8,24},{9,... | collective-permute-start | bytes 737288 | tf_op jit(solution)/shard_map/ppermute | solution.py:295
  107.7 11.1 %collective-permute-start.6 = (bf16[40,3072]{1,0:T(8,128)(2,1)S(1)}, bf16[40,3072]{1,0:T(8,128)(2,1)S(1)}, u32[]{:S(2)}, u32[]{:S(2)}) collective-permute-start(bf16[40,3072]{1,0:T(8,128)(2,1)S(1)} %get-tuple-element.22), channel_id=1, source_target_pairs={{0,16},{1,17},{2,18},{3,19},{4,20},{5,21},{6,22},{7,23},{8,24},{9,... | collective-permute-start | bytes 737288 | tf_op jit(solution)/shard_map/ppermute | solution.py:295
  112.6 9.4 %collective-permute-start.39 = (bf16[40,3072]{1,0:T(8,128)(2,1)S(1)}, bf16[40,3072]{1,0:T(8,128)(2,1)S(1)}, u32[]{:S(2)}, u32[]{:S(2)}) collective-permute-start(bf16[40,3072]{1,0:T(8,128)(2,1)S(1)} %shard_map.126), channel_id=1, source_target_pairs={{0,4},{1,5},{2,6},{3,7},{4,0},{5,1},{6,2},{7,3},{8,12},{9,13},{10,... | collective-permute-start | bytes 737288 | tf_op jit(solution)/shard_map/ppermute | solution.py:295
  115.2 14.4 %collective-permute-start.30 = (bf16[40,3072]{1,0:T(8,128)(2,1)S(1)}, bf16[40,3072]{1,0:T(8,128)(2,1)S(1)}, u32[]{:S(2)}, u32[]{:S(2)}) collective-permute-start(bf16[40,3072]{1,0:T(8,128)(2,1)S(1)} %shard_map.121), channel_id=1, source_target_pairs={{0,8},{1,9},{2,10},{3,11},{4,12},{5,13},{6,14},{7,15},{8,0},{9,1},... | collective-permute-start | bytes 737288 | tf_op jit(solution)/shard_map/ppermute | solution.py:295
  116.1 13.6 %collective-permute-start.20 = (bf16[40,3072]{1,0:T(8,128)(2,1)S(1)}, bf16[40,3072]{1,0:T(8,128)(2,1)S(1)}, u32[]{:S(2)}, u32[]{:S(2)}) collective-permute-start(bf16[40,3072]{1,0:T(8,128)(2,1)S(1)} %shard_map.115), channel_id=1, source_target_pairs={{0,12},{1,13},{2,14},{3,15},{4,8},{5,9},{6,10},{7,11},{8,4},{9,5},... | collective-permute-start | bytes 737288 | tf_op jit(solution)/shard_map/ppermute | solution.py:295
  (24 other events, 211.8 us)

commit v3 on v2

--- a/solution.py
+++ b/solution.py
@@ -32,15 +32,20 @@
 def window_kernel(count, tile, owner_ref, *refs):
     owned = owner_ref[0] == lax.axis_index("rep")
     parts = refs[:count]
-    outs = refs[-count - 2 : -2]
+    outs = refs[-count - 3 : -2]
     rows_ref, hidden_ref = refs[-2:]
-    in_refs, down_ref = refs[count : -count - 3], refs[-count - 3]
+    in_refs, down_ref = refs[count : -count - 4], refs[-count - 4]
     hidden, width = down_ref.shape
     spans = []
     start = 0
     for part in parts:
         spans.append((start, start + part.shape[0]))
         start += part.shape[0]
+    out_spans = []
+    start = 0
+    for out in outs:
+        out_spans.append((start, start + out.shape[0]))
+        start += out.shape[0]
 
     @pl.when(owned)
     def _():
@@ -69,7 +74,7 @@
             sums = jnp.dot(
                 hidden_ref[...], down_ref[:, at : at + wide], preferred_element_type=jnp.float32
             )
-            for out, (low, high) in zip(outs, spans):
+            for out, (low, high) in zip(outs, out_spans):
                 out[:, at : at + wide] = sums[low:high, :].astype(out.dtype)
 
     @pl.when(jnp.logical_not(owned))
@@ -80,15 +85,19 @@
 
 def window(owner, parts, inner, outer):
     count = len(parts)
+    block = parts[-1].shape[0]
+    out_rows = [part.shape[0] for part in parts[:-1]] + [block // 4 * 3, block // 4]
     rows = sum(part.shape[0] for part in parts)
     hidden, width = outer.shape
     tile = 256 if hidden % 256 == 0 else 128
     vmem = pl.BlockSpec(memory_space=pltpu.VMEM)
     return pl.pallas_call(
         functools.partial(window_kernel, count, tile),
-        out_shape=[jax.ShapeDtypeStruct(part.shape, part.dtype) for part in parts],
+        out_shape=[
+            jax.ShapeDtypeStruct((size, width), parts[0].dtype) for size in out_rows
+        ],
         in_specs=[pl.BlockSpec(memory_space=pltpu.SMEM)] + [vmem] * (count + len(inner) + 1),
-        out_specs=[vmem] * count,
+        out_specs=[vmem] * len(out_rows),
         scratch_shapes=[
             pltpu.VMEM((rows, width), jnp.bfloat16),
             pltpu.VMEM((rows, hidden), jnp.bfloat16),
@@ -159,7 +168,7 @@
 
 def far_kernel(part_ref, back_ref, out_ref):
     low = 3 * out_ref.shape[0]
-    out_ref[...] = add_f32(part_ref[low:], back_ref[low:]).astype(out_ref.dtype)
+    out_ref[...] = add_f32(part_ref[low:], back_ref[...]).astype(out_ref.dtype)
 
 
 def near_kernel(part_ref, back_ref, far_ref, x_ref, y_ref):
@@ -348,9 +357,10 @@
         far = to_turn(turn)
         block = local(stack_kernel, (mine, from_x, from_y, far), [(4 * size, width)])
         other = to_core(block)
-        part, part_other = window(owner, [block, other], inner, outer)
-        back = to_core(part_other)
-        far = local(far_kernel, (part, back), [(size, width)])
+        part, part_near, part_far = window(owner, [block, other], inner, outer)
+        back_far = to_core(part_far)
+        back = to_core(part_near)
+        far = local(far_kernel, (part, back_far), [(size, width)])
         far = to_turn(far)
         x_sum, y_sum = local(near_kernel, (part, back, far), [(size, width)] * 2)
         x_sum = to_x(x_sum)

time: 143 us -> 145 us (1.014)
  waiting for transfers between devices: 58.7 us -> 53.7 us
  starting transfers between devices: 37.9 us -> 41.6 us
  local copies, waits for them, and re-layouts: 1.81 us -> 4.3 us
  blocking collectives: 10.8 us -> 13.1 us
    ppermute x40 -> x44, waiting for transfers between devices: 58.7 us -> 53.7 us  [permute(): return lax.ppermute(value, AXES, moves)]
    ppermute x40 -> x44, starting transfers between devices: 37.9 us -> 41.6 us  [permute(): return lax.ppermute(value, AXES, moves)]
    unnamed x16 -> x20, local copies, waits for them, and re-layouts: 1.68 us -> 4.17 us
    all_to_all x1, blocking collectives: 10.8 us -> 13.1 us  [tokens_travel(): totals = jnp.sum(lax.all_to_all(shares, 'mp', 0, 0, tiled=True), axis=0)]
  transfers between devices with their start and end apart: 40 -> 44, of which waited for: 19 -> 17; matrix products, arithmetic and copies ran while one was open for 0% -> 0% of each run, Pallas kernels for 21% -> 20%
where the time goes in v3:
time: 145 us
  waiting for transfers between devices  53.7 us (37%)
  starting transfers between devices  41.6 us (29%)
  Pallas kernels  30 us (21%)
  blocking collectives  13.1 us (9%)
  local copies, waits for them, and re-layouts  4.3 us (3%)
  between operations  1.76 us (1%)
    ppermute x44, waiting for transfers between devices, permute(): return lax.ppermute(value, AXES, moves)  53.7 us
    ppermute x44, starting transfers between devices, permute(): return lax.ppermute(value, AXES, moves)  41.6 us
    pallas_call x4, Pallas kernels, window(): pl.pallas_call(functools.partial(window_kernel, count, tile), out_shape=[...  19.3 us
    all_to_all x1, blocking collectives, tokens_travel(): totals = jnp.sum(lax.all_to_all(shares, 'mp', 0, 0, tiled=True), axis=0)  13.1 us
    pallas_call x4, Pallas kernels, relay(): pl.pallas_call(functools.partial(relay_kernel, start), out_shape=jax.Shap...  7.32 us
    unnamed x20, local copies, waits for them, and re-layouts  4.17 us
  transfers between devices with their start and end apart: 44, of which 17 were waited for; matrix products, arithmetic and copies ran while one was open for 0% of the time, Pallas kernels for 20%

profile of v3, /device:TPU:0, one launch (start us, length us, event | category | flops | bytes accessed | tf_op | source)
XLA Modules:
  0.0 145.0 jit_solution(11886892053124800044)
XLA Ops:
  2.4 3.0 %collective-permute-start = (bf16[40,3072]{1,0:T(8,128)(2,1)S(1)}, bf16[40,3072]{1,0:T(8,128)(2,1)S(1)}, u32[]{:S(2)}, u32[]{:S(2)}) collective-permute-start(bf16[40,3072]{1,0:T(8,128)(2,1)S(1)} %shard_map.104.mine_ref), channel_id=1, source_target_pairs={{0,16},{1,17},{2,18},{3,19},{4,20},{5,21},{6,22},{7,23},{8,24},{9,... | collective-permute-start | bytes 737288 | tf_op jit(solution)/shard_map/ppermute | solution.py:304
  9.2 2.2 %collective-permute-done.x_ref = bf16[40,3072]{1,0:T(8,128)(2,1)S(1)} collective-permute-done((bf16[40,3072]{1,0:T(8,128)(2,1)S(1)}, bf16[40,3072]{1,0:T(8,128)(2,1)S(1)}, u32[]{:S(2)}, u32[]{:S(2)}) %collective-permute-start) | collective-permute-done | bytes 245792 | tf_op jit(solution)/shard_map/ppermute | solution.py:304
  12.9 2.3 %copy-done = bf16[1,768,3072]{2,1,0:T(8,128)(2,1)S(1)} copy-done((bf16[1,768,3072]{2,1,0:T(8,128)(2,1)S(1)}, bf16[1,768,3072]{2,1,0:T(8,128)(2,1)}, u32[]{:S(2)}) %copy-start) | copy-done | bytes 4718616
  20.9 2.3 %collective-permute-done.2.far_ref = bf16[40,3072]{1,0:T(8,128)(2,1)S(1)} collective-permute-done((bf16[40,3072]{1,0:T(8,128)(2,1)S(1)}, bf16[40,3072]{1,0:T(8,128)(2,1)S(1)}, u32[]{:S(2)}, u32[]{:S(2)}) %collective-permute-start.2) | collective-permute-done | bytes 245792 | tf_op jit(solution)/shard_map/ppermute | solution.py:304
  23.3 2.5 %collective-permute-done.34.x_ref = bf16[40,3072]{1,0:T(8,128)(2,1)S(1)} collective-permute-done((bf16[40,3072]{1,0:T(8,128)(2,1)S(1)}, bf16[40,3072]{1,0:T(8,128)(2,1)S(1)}, u32[]{:S(2)}, u32[]{:S(2)}) %collective-permute-start.34) | collective-permute-done | bytes 245792 | tf_op jit(solution)/shard_map/ppermute | solution.py:304
  27.7 2.3 %collective-permute-done.23.end_ref = bf16[40,3072]{1,0:T(8,128)(2,1)S(1)} collective-permute-done((bf16[40,3072]{1,0:T(8,128)(2,1)S(1)}, bf16[40,3072]{1,0:T(8,128)(2,1)S(1)}, u32[]{:S(2)}, u32[]{:S(2)}) %collective-permute-start.23) | collective-permute-done | bytes 245792 | tf_op jit(solution)/shard_map/ppermute | solution.py:304
  30.6 3.0 %collective-permute-done.36.far_ref = bf16[40,3072]{1,0:T(8,128)(2,1)S(1)} collective-permute-done((bf16[40,3072]{1,0:T(8,128)(2,1)S(1)}, bf16[40,3072]{1,0:T(8,128)(2,1)S(1)}, u32[]{:S(2)}, u32[]{:S(2)}) %collective-permute-start.36) | collective-permute-done | bytes 245792 | tf_op jit(solution)/shard_map/ppermute | solution.py:304
  37.8 4.8 %collective-permute-done.25.y_ref = bf16[40,3072]{1,0:T(8,128)(2,1)S(1)} collective-permute-done((bf16[40,3072]{1,0:T(8,128)(2,1)S(1)}, bf16[40,3072]{1,0:T(8,128)(2,1)S(1)}, u32[]{:S(2)}, u32[]{:S(2)}) %collective-permute-start.25) | collective-permute-done | bytes 245792 | tf_op jit(solution)/shard_map/ppermute | solution.py:304
  43.7 4.2 %collective-permute-done.14.y_ref = bf16[40,3072]{1,0:T(8,128)(2,1)S(1)} collective-permute-done((bf16[40,3072]{1,0:T(8,128)(2,1)S(1)}, bf16[40,3072]{1,0:T(8,128)(2,1)S(1)}, u32[]{:S(2)}, u32[]{:S(2)}) %collective-permute-start.14) | collective-permute-done | bytes 245792 | tf_op jit(solution)/shard_map/ppermute | solution.py:304
  57.9 4.8 %window.4 = (bf16[160,3072]{1,0:T(8,128)(2,1)S(1)}, bf16[120,3072]{1,0:T(8,128)(2,1)S(1)}, bf16[40,3072]{1,0:T(8,128)(2,1)S(1)}) custom-call(s32[1]{0:T(128)S(6)} %copy.13.owner_ref, bf16[160,3072]{1,0:T(8,128)(2,1)S(1)} %shard_map.106.refs_0_, bf16[160,3072]{1,0:T(8,128)(2,1)S(1)} %collective-permute-done.3.refs_1_, bf16[768,1536]{1,0:T(8,128)(2,1)S(1)} %relay.4.refs_2_, ...), custom_call_target="tpu_custom_call" | custom-call | flops 4529848320 | bytes 3932160 | tf_op jit(solution)/shard_map/window/pallas_call | solution.py:94
  62.8 5.0 %window.7 = (bf16[160,3072]{1,0:T(8,128)(2,1)S(1)}, bf16[120,3072]{1,0:T(8,128)(2,1)S(1)}, bf16[40,3072]{1,0:T(8,128)(2,1)S(1)}) custom-call(s32[1]{0:T(128)S(6)} %copy.13.owner_ref, bf16[160,3072]{1,0:T(8,128)(2,1)S(1)} %shard_map.123.refs_0_, bf16[160,3072]{1,0:T(8,128)(2,1)S(1)} %collective-permute-done.37.refs_1_, bf16[768,1536]{1,0:T(8,128)(2,1)S(1)} %relay.4.refs_2_, ...), custom_call_target="tpu_custom_call" | custom-call | flops 4529848320 | bytes 3932160 | tf_op jit(solution)/shard_map/window/pallas_call | solution.py:94
  70.6 4.8 %window.6 = (bf16[160,3072]{1,0:T(8,128)(2,1)S(1)}, bf16[120,3072]{1,0:T(8,128)(2,1)S(1)}, bf16[40,3072]{1,0:T(8,128)(2,1)S(1)}) custom-call(s32[1]{0:T(128)S(6)} %copy.13.owner_ref, bf16[160,3072]{1,0:T(8,128)(2,1)S(1)} %shard_map.118.refs_0_, bf16[160,3072]{1,0:T(8,128)(2,1)S(1)} %collective-permute-done.27.refs_1_, bf16[768,1536]{1,0:T(8,128)(2,1)S(1)} %relay.4.refs_2_, ...), custom_call_target="tpu_custom_call" | custom-call | flops 4529848320 | bytes 3932160 | tf_op jit(solution)/shard_map/window/pallas_call | solution.py:94
  76.0 4.8 %window.5 = (bf16[160,3072]{1,0:T(8,128)(2,1)S(1)}, bf16[120,3072]{1,0:T(8,128)(2,1)S(1)}, bf16[40,3072]{1,0:T(8,128)(2,1)S(1)}) custom-call(s32[1]{0:T(128)S(6)} %copy.13.owner_ref, bf16[160,3072]{1,0:T(8,128)(2,1)S(1)} %shard_map.112.refs_0_, bf16[160,3072]{1,0:T(8,128)(2,1)S(1)} %collective-permute-done.16.refs_1_, bf16[768,1536]{1,0:T(8,128)(2,1)S(1)} %relay.4.refs_2_, ...), custom_call_target="tpu_custom_call" | custom-call | flops 4529848320 | bytes 3932160 | tf_op jit(solution)/shard_map/window/pallas_call | solution.py:94
  81.5 3.0 %collective-permute-done.18.back_ref = bf16[40,3072]{1,0:T(8,128)(2,1)S(1)} collective-permute-done((bf16[40,3072]{1,0:T(8,128)(2,1)S(1)}, bf16[40,3072]{1,0:T(8,128)(2,1)S(1)}, u32[]{:S(2)}, u32[]{:S(2)}) %collective-permute-start.18) | collective-permute-done | bytes 245792 | tf_op jit(solution)/shard_map/ppermute | solution.py:304
  86.8 3.9 %collective-permute-done.30.far_ref = bf16[40,3072]{1,0:T(8,128)(2,1)S(1)} collective-permute-done((bf16[40,3072]{1,0:T(8,128)(2,1)S(1)}, bf16[40,3072]{1,0:T(8,128)(2,1)S(1)}, u32[]{:S(2)}, u32[]{:S(2)}) %collective-permute-start.30) | collective-permute-done | bytes 245792 | tf_op jit(solution)/shard_map/ppermute | solution.py:304
  90.7 2.6 %collective-permute-start.42 = (bf16[40,3072]{1,0:T(8,128)(2,1)S(1)}, bf16[40,3072]{1,0:T(8,128)(2,1)S(1)}, u32[]{:S(2)}, u32[]{:S(2)}) collective-permute-start(bf16[40,3072]{1,0:T(8,128)(2,1)S(1)} %get-tuple-element.43), channel_id=1, source_target_pairs={{0,2},{1,3},{2,0},{3,1},{4,6},{5,7},{6,4},{7,5},{8,10},{9,11},{10,... | collective-permute-start | bytes 737288 | tf_op jit(solution)/shard_map/ppermute | solution.py:304
  94.1 2.6 %collective-permute-start.32 = (bf16[40,3072]{1,0:T(8,128)(2,1)S(1)}, bf16[40,3072]{1,0:T(8,128)(2,1)S(1)}, u32[]{:S(2)}, u32[]{:S(2)}) collective-permute-start(bf16[40,3072]{1,0:T(8,128)(2,1)S(1)} %get-tuple-element.38), channel_id=1, source_target_pairs={{0,2},{1,3},{2,0},{3,1},{4,6},{5,7},{6,4},{7,5},{8,10},{9,11},{10,... | collective-permute-start | bytes 737288 | tf_op jit(solution)/shard_map/ppermute | solution.py:304
  96.9 2.6 %collective-permute-done.41.x_ref = bf16[40,3072]{1,0:T(8,128)(2,1)S(1)} collective-permute-done((bf16[40,3072]{1,0:T(8,128)(2,1)S(1)}, bf16[40,3072]{1,0:T(8,128)(2,1)S(1)}, u32[]{:S(2)}, u32[]{:S(2)}) %collective-permute-start.41) | collective-permute-done | bytes 245792 | tf_op jit(solution)/shard_map/ppermute | solution.py:304
  100.3 2.1 %collective-permute-start.7 = (bf16[40,3072]{1,0:T(8,128)(2,1)S(1)}, bf16[40,3072]{1,0:T(8,128)(2,1)S(1)}, u32[]{:S(2)}, u32[]{:S(2)}) collective-permute-start(bf16[40,3072]{1,0:T(8,128)(2,1)S(1)} %get-tuple-element.27), channel_id=1, source_target_pairs={{0,16},{1,17},{2,18},{3,19},{4,20},{5,21},{6,22},{7,23},{8,24},{9,... | collective-permute-start | bytes 737288 | tf_op jit(solution)/shard_map/ppermute | solution.py:304
  102.5 2.3 %collective-permute-done.31.x_ref = bf16[40,3072]{1,0:T(8,128)(2,1)S(1)} collective-permute-done((bf16[40,3072]{1,0:T(8,128)(2,1)S(1)}, bf16[40,3072]{1,0:T(8,128)(2,1)S(1)}, u32[]{:S(2)}, u32[]{:S(2)}) %collective-permute-start.31) | collective-permute-done | bytes 245792 | tf_op jit(solution)/shard_map/ppermute | solution.py:304
  107.3 2.8 %collective-permute-done.20.x_ref = bf16[40,3072]{1,0:T(8,128)(2,1)S(1)} collective-permute-done((bf16[40,3072]{1,0:T(8,128)(2,1)S(1)}, bf16[40,3072]{1,0:T(8,128)(2,1)S(1)}, u32[]{:S(2)}, u32[]{:S(2)}) %collective-permute-start.20) | collective-permute-done | bytes 245792 | tf_op jit(solution)/shard_map/ppermute | solution.py:304
  112.1 2.8 %collective-permute-start.22 = (bf16[40,3072]{1,0:T(8,128)(2,1)S(1)}, bf16[40,3072]{1,0:T(8,128)(2,1)S(1)}, u32[]{:S(2)}, u32[]{:S(2)}) collective-permute-start(bf16[40,3072]{1,0:T(8,128)(2,1)S(1)} %shard_map.115), channel_id=1, source_target_pairs={{0,12},{1,13},{2,14},{3,15},{4,8},{5,9},{6,10},{7,11},{8,4},{9,5},... | collective-permute-start | bytes 737288 | tf_op jit(solution)/shard_map/ppermute | solution.py:304
  115.0 14.6 %collective-permute-done.33.refs_2_ = bf16[40,3072]{1,0:T(8,128)(2,1)S(1)} collective-permute-done((bf16[40,3072]{1,0:T(8,128)(2,1)S(1)}, bf16[40,3072]{1,0:T(8,128)(2,1)S(1)}, u32[]{:S(2)}, u32[]{:S(2)}) %collective-permute-start.33) | collective-permute-done | bytes 245792 | tf_op jit(solution)/shard_map/ppermute | solution.py:304
  131.4 13.1 %all_to_all.6 = f32[16,1,8]{2,1,0:T(1,128)S(1)} all-to-all(f32[16,1,8]{2,1,0:T(1,128)S(1)} %broadcast_in_dim.20), channel_id=1, replica_groups=mesh['rep'=2,'mp'=16] {'mp'}, dimensions={0} | all-to-all | bytes 1024 | tf_op jit(solution)/shard_map/all_to_all | solution.py:376
  (122 shorter events, 45.1 us)
Async XLA Ops:
  8.6 11.0 %collective-permute-start.9 = (bf16[40,3072]{1,0:T(8,128)(2,1)S(1)}, bf16[40,3072]{1,0:T(8,128)(2,1)S(1)}, u32[]{:S(2)}, u32[]{:S(2)}) collective-permute-start(bf16[40,3072]{1,0:T(8,128)(2,1)S(1)} %shard_map.104.mine_ref), channel_id=1, source_target_pairs={{4,8},{5,9},{6,10},{7,11},{8,4},{9,5},{10,6},{11,7},{20,24},{21,25... | collective-permute-start | bytes 737288 | tf_op jit(solution)/shard_map/ppermute | solution.py:304
  15.7 10.1 %collective-permute-start.34 = (bf16[40,3072]{1,0:T(8,128)(2,1)S(1)}, bf16[40,3072]{1,0:T(8,128)(2,1)S(1)}, u32[]{:S(2)}, u32[]{:S(2)}) collective-permute-start(bf16[40,3072]{1,0:T(8,128)(2,1)S(1)} %collective-permute-done.10.mine_ref), channel_id=1, source_target_pairs={{0,16},{1,17},{2,18},{3,19},{4,20},{5,21},{6,22},{7,23},{8,24},{9,... | collective-permute-start | bytes 737288 | tf_op jit(solution)/shard_map/ppermute | solution.py:304
  19.6 10.5 %collective-permute-start.23 = (bf16[40,3072]{1,0:T(8,128)(2,1)S(1)}, bf16[40,3072]{1,0:T(8,128)(2,1)S(1)}, u32[]{:S(2)}, u32[]{:S(2)}) collective-permute-start(bf16[40,3072]{1,0:T(8,128)(2,1)S(1)} %collective-permute-done.9.middle_ref), channel_id=1, source_target_pairs={{4,0},{5,1},{6,2},{7,3},{8,12},{9,13},{10,14},{11,15},{20,16},{21,... | collective-permute-start | bytes 737288 | tf_op jit(solution)/shard_map/ppermute | solution.py:304
  23.2 34.6 %collective-permute-start.3 = (bf16[160,3072]{1,0:T(8,128)(2,1)S(1)}, bf16[160,3072]{1,0:T(8,128)(2,1)S(1)}, u32[]{:S(2)}, u32[]{:S(2)}) collective-permute-start(bf16[160,3072]{1,0:T(8,128)(2,1)S(1)} %shard_map.106.refs_0_), channel_id=1, source_target_pairs={{0,1},{1,0},{2,3},{3,2},{4,5},{5,4},{6,7},{7,6},{8,9},{9,8},{10,11... | collective-permute-start | bytes 2949128 | tf_op jit(solution)/shard_map/ppermute | solution.py:304
  33.6 29.2 %collective-permute-start.37 = (bf16[160,3072]{1,0:T(8,128)(2,1)S(1)}, bf16[160,3072]{1,0:T(8,128)(2,1)S(1)}, u32[]{:S(2)}, u32[]{:S(2)}) collective-permute-start(bf16[160,3072]{1,0:T(8,128)(2,1)S(1)} %shard_map.123.refs_0_), channel_id=1, source_target_pairs={{0,1},{1,0},{2,3},{3,2},{4,5},{5,4},{6,7},{7,6},{8,9},{9,8},{10,11... | collective-permute-start | bytes 2949128 | tf_op jit(solution)/shard_map/ppermute | solution.py:304
  36.3 11.6 %collective-permute-start.14 = (bf16[40,3072]{1,0:T(8,128)(2,1)S(1)}, bf16[40,3072]{1,0:T(8,128)(2,1)S(1)}, u32[]{:S(2)}, u32[]{:S(2)}) collective-permute-start(bf16[40,3072]{1,0:T(8,128)(2,1)S(1)} %shard_map.110.mine_ref), channel_id=1, source_target_pairs={{0,2},{1,3},{2,0},{3,1},{4,6},{5,7},{6,4},{7,5},{8,10},{9,11},{10,... | collective-permute-start | bytes 737288 | tf_op jit(solution)/shard_map/ppermute | solution.py:304
  42.6 14.4 %collective-permute-start.26 = (bf16[40,3072]{1,0:T(8,128)(2,1)S(1)}, bf16[40,3072]{1,0:T(8,128)(2,1)S(1)}, u32[]{:S(2)}, u32[]{:S(2)}) collective-permute-start(bf16[40,3072]{1,0:T(8,128)(2,1)S(1)} %shard_map.117), channel_id=1, source_target_pairs={{0,16},{1,3},{2,18},{3,1},{4,20},{5,7},{6,22},{7,5},{8,24},{9,11},... | collective-permute-start | bytes 737288 | tf_op jit(solution)/shard_map/ppermute | solution.py:304
  57.1 13.6 %collective-permute-start.27 = (bf16[160,3072]{1,0:T(8,128)(2,1)S(1)}, bf16[160,3072]{1,0:T(8,128)(2,1)S(1)}, u32[]{:S(2)}, u32[]{:S(2)}) collective-permute-start(bf16[160,3072]{1,0:T(8,128)(2,1)S(1)} %shard_map.118.refs_0_), channel_id=1, source_target_pairs={{0,1},{1,0},{2,3},{3,2},{4,5},{5,4},{6,7},{7,6},{8,9},{9,8},{10,11... | collective-permute-start | bytes 2949128 | tf_op jit(solution)/shard_map/ppermute | solution.py:304
  57.2 18.3 %collective-permute-start.16 = (bf16[160,3072]{1,0:T(8,128)(2,1)S(1)}, bf16[160,3072]{1,0:T(8,128)(2,1)S(1)}, u32[]{:S(2)}, u32[]{:S(2)}) collective-permute-start(bf16[160,3072]{1,0:T(8,128)(2,1)S(1)} %shard_map.112.refs_0_), channel_id=1, source_target_pairs={{0,1},{1,0},{2,3},{3,2},{4,5},{5,4},{6,7},{7,6},{8,9},{9,8},{10,11... | collective-permute-start | bytes 2949128 | tf_op jit(solution)/shard_map/ppermute | solution.py:304
  68.1 16.4 %collective-permute-start.38 = (bf16[120,3072]{1,0:T(8,128)(2,1)S(1)}, bf16[120,3072]{1,0:T(8,128)(2,1)S(1)}, u32[]{:S(2)}, u32[]{:S(2)}) collective-permute-start(bf16[120,3072]{1,0:T(8,128)(2,1)S(1)} %get-tuple-element.40), channel_id=1, source_target_pairs={{0,1},{1,0},{2,3},{3,2},{4,5},{5,4},{6,7},{7,6},{8,9},{9,8},{10,11... | collective-permute-start | bytes 2211848 | tf_op jit(solution)/shard_map/ppermute | solution.py:304
  68.4 12.4 %collective-permute-start.6 = (bf16[40,3072]{1,0:T(8,128)(2,1)S(1)}, bf16[40,3072]{1,0:T(8,128)(2,1)S(1)}, u32[]{:S(2)}, u32[]{:S(2)}) collective-permute-start(bf16[40,3072]{1,0:T(8,128)(2,1)S(1)} %shard_map.107), channel_id=1, source_target_pairs={{0,16},{1,3},{2,18},{3,1},{4,20},{5,7},{6,22},{7,5},{8,24},{9,11},... | collective-permute-start | bytes 737288 | tf_op jit(solution)/shard_map/ppermute | solution.py:304
  69.4 11.5 %collective-permute-start.40 = (bf16[40,3072]{1,0:T(8,128)(2,1)S(1)}, bf16[40,3072]{1,0:T(8,128)(2,1)S(1)}, u32[]{:S(2)}, u32[]{:S(2)}) collective-permute-start(bf16[40,3072]{1,0:T(8,128)(2,1)S(1)} %shard_map.124), channel_id=1, source_target_pairs={{0,16},{1,3},{2,18},{3,1},{4,20},{5,7},{6,22},{7,5},{8,24},{9,11},... | collective-permute-start | bytes 737288 | tf_op jit(solution)/shard_map/ppermute | solution.py:304
  75.5 15.2 %collective-permute-start.28 = (bf16[120,3072]{1,0:T(8,128)(2,1)S(1)}, bf16[120,3072]{1,0:T(8,128)(2,1)S(1)}, u32[]{:S(2)}, u32[]{:S(2)}) collective-permute-start(bf16[120,3072]{1,0:T(8,128)(2,1)S(1)} %get-tuple-element.35), channel_id=1, source_target_pairs={{0,1},{1,0},{2,3},{3,2},{4,5},{5,4},{6,7},{7,6},{8,9},{9,8},{10,11... | collective-permute-start | bytes 2211848 | tf_op jit(solution)/shard_map/ppermute | solution.py:304
  80.8 13.3 %collective-permute-start.17 = (bf16[120,3072]{1,0:T(8,128)(2,1)S(1)}, bf16[120,3072]{1,0:T(8,128)(2,1)S(1)}, u32[]{:S(2)}, u32[]{:S(2)}) collective-permute-start(bf16[120,3072]{1,0:T(8,128)(2,1)S(1)} %get-tuple-element.30), channel_id=1, source_target_pairs={{0,1},{1,0},{2,3},{3,2},{4,5},{5,4},{6,7},{7,6},{8,9},{9,8},{10,11... | collective-permute-start | bytes 2211848 | tf_op jit(solution)/shard_map/ppermute | solution.py:304
  81.0 15.9 %collective-permute-start.4 = (bf16[120,3072]{1,0:T(8,128)(2,1)S(1)}, bf16[120,3072]{1,0:T(8,128)(2,1)S(1)}, u32[]{:S(2)}, u32[]{:S(2)}) collective-permute-start(bf16[120,3072]{1,0:T(8,128)(2,1)S(1)} %get-tuple-element.25), channel_id=1, source_target_pairs={{0,1},{1,0},{2,3},{3,2},{4,5},{5,4},{6,7},{7,6},{8,9},{9,8},{10,11... | collective-permute-start | bytes 2211848 | tf_op jit(solution)/shard_map/ppermute | solution.py:304
  94.1 10.7 %collective-permute-start.31 = (bf16[40,3072]{1,0:T(8,128)(2,1)S(1)}, bf16[40,3072]{1,0:T(8,128)(2,1)S(1)}, u32[]{:S(2)}, u32[]{:S(2)}) collective-permute-start(bf16[40,3072]{1,0:T(8,128)(2,1)S(1)} %get-tuple-element.37), channel_id=1, source_target_pairs={{0,16},{1,17},{2,18},{3,19},{4,20},{5,21},{6,22},{7,23},{8,24},{9,... | collective-permute-start | bytes 737288 | tf_op jit(solution)/shard_map/ppermute | solution.py:304
  94.1 11.3 %collective-permute-start.32 = (bf16[40,3072]{1,0:T(8,128)(2,1)S(1)}, bf16[40,3072]{1,0:T(8,128)(2,1)S(1)}, u32[]{:S(2)}, u32[]{:S(2)}) collective-permute-start(bf16[40,3072]{1,0:T(8,128)(2,1)S(1)} %get-tuple-element.38), channel_id=1, source_target_pairs={{0,2},{1,3},{2,0},{3,1},{4,6},{5,7},{6,4},{7,5},{8,10},{9,11},{10,... | collective-permute-start | bytes 737288 | tf_op jit(solution)/shard_map/ppermute | solution.py:304
  96.8 13.2 %collective-permute-start.20 = (bf16[40,3072]{1,0:T(8,128)(2,1)S(1)}, bf16[40,3072]{1,0:T(8,128)(2,1)S(1)}, u32[]{:S(2)}, u32[]{:S(2)}) collective-permute-start(bf16[40,3072]{1,0:T(8,128)(2,1)S(1)} %get-tuple-element.32), channel_id=1, source_target_pairs={{0,16},{1,17},{2,18},{3,19},{4,20},{5,21},{6,22},{7,23},{8,24},{9,... | collective-permute-start | bytes 737288 | tf_op jit(solution)/shard_map/ppermute | solution.py:304
  99.5 12.5 %collective-permute-start.21 = (bf16[40,3072]{1,0:T(8,128)(2,1)S(1)}, bf16[40,3072]{1,0:T(8,128)(2,1)S(1)}, u32[]{:S(2)}, u32[]{:S(2)}) collective-permute-start(bf16[40,3072]{1,0:T(8,128)(2,1)S(1)} %get-tuple-element.33), channel_id=1, source_target_pairs={{0,2},{1,3},{2,0},{3,1},{4,6},{5,7},{6,4},{7,5},{8,10},{9,11},{10,... | collective-permute-start | bytes 737288 | tf_op jit(solution)/shard_map/ppermute | solution.py:304
  100.3 14.6 %collective-permute-start.7 = (bf16[40,3072]{1,0:T(8,128)(2,1)S(1)}, bf16[40,3072]{1,0:T(8,128)(2,1)S(1)}, u32[]{:S(2)}, u32[]{:S(2)}) collective-permute-start(bf16[40,3072]{1,0:T(8,128)(2,1)S(1)} %get-tuple-element.27), channel_id=1, source_target_pairs={{0,16},{1,17},{2,18},{3,19},{4,20},{5,21},{6,22},{7,23},{8,24},{9,... | collective-permute-start | bytes 737288 | tf_op jit(solution)/shard_map/ppermute | solution.py:304
  104.8 10.1 %collective-permute-start.8 = (bf16[40,3072]{1,0:T(8,128)(2,1)S(1)}, bf16[40,3072]{1,0:T(8,128)(2,1)S(1)}, u32[]{:S(2)}, u32[]{:S(2)}) collective-permute-start(bf16[40,3072]{1,0:T(8,128)(2,1)S(1)} %get-tuple-element.28), channel_id=1, source_target_pairs={{0,2},{1,3},{2,0},{3,1},{4,6},{5,7},{6,4},{7,5},{8,10},{9,11},{10,... | collective-permute-start | bytes 737288 | tf_op jit(solution)/shard_map/ppermute | solution.py:304
  105.4 9.6 %collective-permute-start.43 = (bf16[40,3072]{1,0:T(8,128)(2,1)S(1)}, bf16[40,3072]{1,0:T(8,128)(2,1)S(1)}, u32[]{:S(2)}, u32[]{:S(2)}) collective-permute-start(bf16[40,3072]{1,0:T(8,128)(2,1)S(1)} %shard_map.126), channel_id=1, source_target_pairs={{0,4},{1,5},{2,6},{3,7},{4,0},{5,1},{6,2},{7,3},{8,12},{9,13},{10,... | collective-permute-start | bytes 737288 | tf_op jit(solution)/shard_map/ppermute | solution.py:304
  110.0 19.6 %collective-permute-start.33 = (bf16[40,3072]{1,0:T(8,128)(2,1)S(1)}, bf16[40,3072]{1,0:T(8,128)(2,1)S(1)}, u32[]{:S(2)}, u32[]{:S(2)}) collective-permute-start(bf16[40,3072]{1,0:T(8,128)(2,1)S(1)} %shard_map.121), channel_id=1, source_target_pairs={{0,8},{1,9},{2,10},{3,11},{4,12},{5,13},{6,14},{7,15},{8,0},{9,1},... | collective-permute-start | bytes 737288 | tf_op jit(solution)/shard_map/ppermute | solution.py:304
  112.1 17.5 %collective-permute-start.22 = (bf16[40,3072]{1,0:T(8,128)(2,1)S(1)}, bf16[40,3072]{1,0:T(8,128)(2,1)S(1)}, u32[]{:S(2)}, u32[]{:S(2)}) collective-permute-start(bf16[40,3072]{1,0:T(8,128)(2,1)S(1)} %shard_map.115), channel_id=1, source_target_pairs={{0,12},{1,13},{2,14},{3,15},{4,8},{5,9},{6,10},{7,11},{8,4},{9,5},... | collective-permute-start | bytes 737288 | tf_op jit(solution)/shard_map/ppermute | solution.py:304
  (30 other events, 272.4 us)
